TPU v7x, 32 devices: a whole 2x2x4 slice. The times are simulated.
32 devices in a mesh: lat: 4 (over y, core), lon: 8 (over z, x).
Axes of the slice: x: 2, y: 2, z: 4, core: 2. Of those that a mesh axis runs over, the one named last changes fastest.
Arguments:
- forcing: float32 [640, 1024], P('lat', 'lon'), may hold values from -28 to 28
- search_direction: float32 [640, 1024], P('lat', 'lon'), may hold values from -28 to 28
- ocean_depth: float32 [640, 1024], P('lat', 'lon'), may hold values from 0.5 to 8
- land_mask: int32 [640, 1024], P('lat', 'lon'), may hold values 0 or 1
- fold_map: int32 [1024], replicated, may hold values from 0 to 1023, as said below
Outputs:
- scaled_height: float32 [640, 1024], P('lat', 'lon')
- residual: float32 [640, 1024], P('lat', 'lon')
Inputs may be any that keep to these rules, and one draw needn't show every extreme that they name: `fold_map`: column j's partner across the fold is (c - j) mod 1024 for one c of 0 to 1023, so the map is its own inverse.
All inputs are finite; a program needn't handle non-finite values. No bound on the sum of `land_mask` on one device may be relied on, other than what follows from the above.
Results may differ from a plain program's by a relative error of at most 0.0003.
Values sent between devices are 32-bit elements; how exact they have to be, the bound alone decides.
A program may use at most 64 MiB of HBM per device.

v0:
```python
import functools

import jax
import jax.numpy as jnp
from jax import lax
from jax.experimental import pallas as pl
from jax.experimental.pallas import tpu as pltpu
from jax.sharding import PartitionSpec as P

STEPS = 8
REACH = 256
MESH = pl.DeviceIdType.MESH
PAD = 16
GROUP = 32
CHUNK = 16
DIRECT_LIMIT = 64

DIRECTIONS = ((1, 0), (-1, 0), (0, 1), (0, -1), (1, 1), (-1, -1), (1, -1), (-1, 1))
SLOT = {offset: index for index, offset in enumerate(DIRECTIONS)}


def halves(offset):
    return 0.5 if 0 in offset else 0.25


def chunks_of(low, high, size):
    return [(at, min(size, high - at)) for at in range(low, high, size)]


def shift_pair(centre, halo, step):
    width = centre.shape[1]
    lane = lax.broadcasted_iota(jnp.int32, centre.shape, 1)
    edge = lane == (0 if step == 1 else width - 1)
    turn = width - 1 if step == 1 else 1
    return (
        pltpu.roll(jnp.where(edge, halo, centre), turn, 1),
        pltpu.roll(jnp.where(edge, centre, halo), turn, 1),
    )


def turned(x, shift):
    shift = shift % x.shape[1]
    return x if shift == 0 else pltpu.roll(x, shift, 1)


def bilinear(left, right, gram):
    total = None
    for i in sorted(left):
        inner = None
        for j in sorted(right):
            term = gram(i, j) * right[j]
            inner = term if inner is None else inner + term
        inner = left[i] * inner
        total = inner if total is None else total + inner
    return total


def plus(left, right):
    result = dict(left)
    for key, value in right.items():
        result[key] = result[key] + value if key in result else value
    return result


def scaled(factor, vector):
    return {key: factor * value for key, value in vector.items()}


def apply_shift(vector):
    result = {}
    for (chain, power), value in vector.items():
        parts = [((chain, power), value)]
        if power == 0:
            parts.append(((chain, 1), value))
        else:
            half = 0.5 * value
            parts += [((chain, power + 1), half), ((chain, power - 1), half)]
        result = plus(result, {}) if not parts else result
        for key, part in parts:
            result = plus(result, {key: part})
    return result


def coordinates(moments):
    cache = {}

    def gram(left, right):
        kind = (left[0], right[0]) if left[0] <= right[0] else (right[0], left[0])
        low, high = sorted((left[1], right[1]))
        key = (kind, low, high)
        if key not in cache:
            series = moments[kind]
            cache[key] = 0.5 * (series[high + low] + series[high - low])
        return cache[key]

    solution_coords = {}
    one = jnp.ones_like(moments[("p", "p")][0])
    direction_coords = {("p", 0): one}
    residual_coords = {("r", 0): one}
    norm_now = bilinear(residual_coords, residual_coords, gram)
    for _ in range(STEPS):
        mapped = apply_shift(direction_coords)
        step_length = norm_now / bilinear(direction_coords, mapped, gram)
        solution_coords = plus(solution_coords, scaled(step_length, direction_coords))
        residual_coords = plus(residual_coords, scaled(-step_length, mapped))
        norm_next = bilinear(residual_coords, residual_coords, gram)
        direction_coords = plus(
            residual_coords, scaled(norm_next / norm_now, direction_coords)
        )
        norm_now = norm_next
    return solution_coords, residual_coords


def fold_sublanes(parts):
    row = lax.broadcasted_iota(jnp.int32, parts[0].shape, 0)
    parts = list(parts)
    span = 4
    while span:
        low = (row & span) == 0
        half = len(parts) // 2
        parts = [
            jnp.where(low, first, second)
            + pltpu.roll(jnp.where(low, second, first), span, 0)
            if span == 4
            else jnp.where(low, first, second)
            + jnp.where(low, pltpu.roll(first, 8 - span, 0), pltpu.roll(second, span, 0))
            for first, second in zip(parts[:half], parts[half:])
        ]
        span //= 2
    return parts[0]


def kernel(
    n_lat, n_lon, forcing_hbm, search_hbm, depth_hbm, mask_hbm, fold_hbm,
    out_height, out_residual, forcing, search, depth_in, mask_in, fold_map,
    depth, depth_e, depth_w, root, root_e, root_w, weights, basis, basis_halo,
    row_north, row_south, fold_rows, packed, got_north, got_south, got_east, got_west,
    corners, fold_all, dots, sums_lat, sums_lon, sums_all, moment_rows, load_sem,
    near_send, near_recv, fold_send, fold_recv, lat_send, lat_recv, lon_send, lon_recv,
    all_send, all_recv,
):
    rows, width = forcing_hbm.shape
    lat, lon = lax.axis_index("lat"), lax.axis_index("lon")
    top = n_lat - 1
    north, south = lax.rem(lat + 1, n_lat), lax.rem(lat + n_lat - 1, n_lat)
    east, west = lax.rem(lon + 1, n_lon), lax.rem(lon + n_lon - 1, n_lon)
    has_north, has_south = lat < top, lat > 0
    group_rows = rows * GROUP // width
    n_groups = width // GROUP

    barrier = pltpu.get_barrier_semaphore()

    def greet(place):
        pl.semaphore_signal(barrier, inc=1, device_id=place, device_id_type=MESH)

    loads = [
        pltpu.make_async_copy(source, target, load_sem.at[index])
        for index, (source, target) in enumerate(
            ((mask_hbm, mask_in), (depth_hbm, depth_in), (search_hbm, search),
             (forcing_hbm, forcing), (fold_hbm, fold_map))
        )
    ]
    for load in loads:
        load.start()
    direct = n_lat * n_lon <= DIRECT_LIMIT
    everyone = [(a, b) for a in range(n_lat) for b in range(n_lon) if a or b]
    everyone.sort(key=lambda d: -min(d[0], n_lat - d[0]) - min(d[1], n_lon - d[1]))
    if direct:
        for a, b in everyone:
            greet((lax.rem(lat + a, n_lat), lax.rem(lon + b, n_lon)))
        greeted = len(everyone)
    else:
        for d in range(1, n_lat):
            greet((lax.rem(lat + d, n_lat), lon))
        for d in range(1, n_lon):
            greet((lat, lax.rem(lon + d, n_lon)))
        for place in ((north, east), (north, west), (south, east), (south, west)):
            greet(place)
        greeted = n_lat - 1 + n_lon - 1 + 4

    for load in loads:
        load.wait()
    lane_group = lax.broadcasted_iota(jnp.int32, (group_rows, width), 1)
    west_edge = east_edge = None
    for g in range(n_groups):
        here = pl.ds(g * group_rows, group_rows)
        there = pl.ds(PAD + g * group_rows, group_rows)
        flag = mask_in[here, :].astype(jnp.float32)
        deep = depth_in[here, :] * flag
        moving = search[here, :] * flag
        left = forcing[here, :] * flag
        depth[0, there, :] = deep
        basis[0, there, :] = moving
        basis[STEPS + 1, there, :] = left
        inside = lane_group - g * GROUP
        to_west = jnp.where(
            inside < 9,
            turned(deep, g * GROUP),
            jnp.where(inside < 17, turned(moving, g * GROUP + 9), turned(left, g * GROUP + 17)),
        )
        to_east = jnp.where(
            inside < 9,
            turned(deep, g * GROUP + 9),
            jnp.where(inside < 17, turned(moving, g * GROUP + 17), turned(left, g * GROUP + 25)),
        )
        west_edge = to_west if g == 0 else jnp.where(inside >= 0, to_west, west_edge)
        east_edge = to_east if g == 0 else jnp.where(inside >= 0, to_east, east_edge)
    packed[0] = west_edge
    packed[1] = east_edge
    first, last = PAD, PAD + rows
    row_south[0:16, :] = depth[0, first : first + 16, :]
    row_south[16:24, :] = basis[0, first : first + 8, :]
    row_south[24:32, :] = basis[STEPS + 1, first : first + 8, :]
    row_north[0:16, :] = depth[0, last - 16 : last, :]
    row_north[16:24, :] = basis[0, last - 8 : last, :]
    row_north[24:32, :] = basis[STEPS + 1, last - 8 : last, :]

    @pl.when(lat == top)
    def _():
        for r in range(16):
            fold_rows[r : r + 1, :] = depth[0, last - 1 - r : last - r, :]
        for r in range(8):
            fold_rows[16 + r : 17 + r, :] = basis[0, last - 1 - r : last - r, :]
            fold_rows[24 + r : 25 + r, :] = basis[STEPS + 1, last - 1 - r : last - r, :]
        fold_all[lon] = fold_rows[...]

    pl.semaphore_wait(barrier, greeted)

    def near(index, source, target, place):
        return pltpu.make_async_remote_copy(
            src_ref=source, dst_ref=target, send_sem=near_send.at[index],
            recv_sem=near_recv.at[index], device_id=place, device_id_type=MESH,
        )

    tail = pl.ds(group_rows - 16, 16)
    head = pl.ds(0, 16)
    to_north = near(0, row_north, got_south, (north, lon))
    to_south = near(1, row_south, got_north, (south, lon))
    to_east = near(2, packed.at[1], got_west, (lat, east))
    to_west = near(3, packed.at[0], got_east, (lat, west))
    to_ne = near(4, packed.at[1, tail], corners.at[0], (north, east))
    to_nw = near(5, packed.at[0, tail], corners.at[1], (north, west))
    to_se = near(6, packed.at[1, head], corners.at[2], (south, east))
    to_sw = near(7, packed.at[0, head], corners.at[3], (south, west))
    northward, southward = (to_north, to_ne, to_nw), (to_south, to_se, to_sw)

    def spread(source, slots, send_sem, recv_sem, along_lat):
        size = n_lat if along_lat else n_lon
        me = lat if along_lat else lon
        copies = []
        for d in range(1, size):
            peer = lax.rem(me + d, size)
            copies.append(
                pltpu.make_async_remote_copy(
                    src_ref=source, dst_ref=slots.at[me], send_sem=send_sem.at[d - 1],
                    recv_sem=recv_sem.at[d - 1],
                    device_id=(peer, lon) if along_lat else (lat, peer),
                    device_id_type=MESH,
                )
            )
        return copies

    across = spread(fold_rows, fold_all, fold_send, fold_recv, False)

    @pl.when(lat == top)
    def _():
        for copy in across:
            copy.start()

    to_east.start()
    to_west.start()

    @pl.when(has_north)
    def _():
        for copy in northward:
            copy.start()

    @pl.when(has_south)
    def _():
        for copy in southward:
            copy.start()

    def unpack(got_e, got_w, start, g, count):
        lane = lax.broadcasted_iota(jnp.int32, (count, width), 1)
        base = -g * GROUP
        spans = ((0, 9, depth.at[1]), (9, 8, basis_halo.at[0]), (17, 8, basis_halo.at[STEPS + 1]))
        for offset, cells, target in spans:
            from_east = turned(got_e, base - offset)
            from_west = turned(got_w, base - offset - cells)
            target[start : start + count, :] = jnp.where(
                lane < cells,
                from_east,
                jnp.where(lane >= width - cells, from_west, jnp.zeros_like(got_e)),
            )

    to_east.wait_recv()
    to_west.wait_recv()
    for g in range(n_groups):
        unpack(got_east[...], got_west[...], PAD + g * group_rows, g, group_rows)

    @pl.when(has_south)
    def _():
        for copy in northward:
            copy.wait_recv()
        depth[0, 0:16, :] = got_south[0:16, :]
        basis[0, 8:16, :] = got_south[16:24, :]
        basis[STEPS + 1, 8:16, :] = got_south[24:32, :]
        unpack(corners[1], corners[0], 0, n_groups - 1, 16)

    @pl.when(lat == 0)
    def _():
        nothing = jnp.zeros((16, width), jnp.float32)
        for target in (depth.at[0], depth.at[1]):
            target[0:16, :] = nothing
        for power in (0, STEPS + 1):
            basis[power, 0:16, :] = nothing
            basis_halo[power, 0:16, :] = nothing

    @pl.when(has_north)
    def _():
        for copy in southward:
            copy.wait_recv()
        depth[0, last : last + 16, :] = got_north[0:16, :]
        basis[0, last : last + 8, :] = got_north[16:24, :]
        basis[STEPS + 1, last : last + 8, :] = got_north[24:32, :]
        unpack(corners[3], corners[2], last, 0, 16)

    @pl.when(lat == top)
    def _():
        for copy in across:
            copy.wait_recv()
        total = n_lon * width
        pivot = lax.rem(fold_map[0] - lon * width + total, total)
        block, offset = pivot // width, lax.rem(pivot, width)
        lane = lax.broadcasted_iota(jnp.int32, (32, width), 1)
        index = lax.rem(offset - lane + width, width)

        def mirrored(which):
            rows_of = fold_all[lax.rem(block + which + n_lon, n_lon)]
            return jnp.take_along_axis(rows_of, index, axis=1, mode="promise_in_bounds")

        ahead, same, behind, beyond = (mirrored(which) for which in (1, 0, -1, -2))
        close = lane <= offset
        centre = jnp.where(close, same, behind)
        halo = jnp.where(
            lane < width // 2, jnp.where(close, behind, beyond), jnp.where(close, ahead, same)
        )
        for value, deep, fields in ((centre, depth.at[0], basis), (halo, depth.at[1], basis_halo)):
            deep[last : last + 16, :] = value[0:16, :]
            fields[0, last : last + 8, :] = value[16:24, :]
            fields[STEPS + 1, last : last + 8, :] = value[24:32, :]

    low, high = PAD - 8, last + 8
    for at, count in chunks_of(0, rows + 2 * PAD, CHUNK):
        span = pl.ds(at, count)
        centre, halo = depth[0, span, :], depth[1, span, :]
        depth_e[0, span, :], depth_e[1, span, :] = shift_pair(centre, halo, 1)
        depth_w[0, span, :], depth_w[1, span, :] = shift_pair(centre, halo, -1)
    shifted_depth = {0: depth, 1: depth_e, -1: depth_w}
    for at, count in chunks_of(low, high, CHUNK):
        roots = []
        for tile in (0, 1):
            here = depth[tile, at : at + count, :]
            sums = {0.5: None, 0.25: None}
            for a, b in DIRECTIONS:
                beside = shifted_depth[b][tile, at + a : at + a + count, :]
                link = jnp.where(beside > 0.0, here + beside, 0.0)
                factor = halves((a, b))
                sums[factor] = link if sums[factor] is None else sums[factor] + link
            diagonal = here * (1.0 / (REACH * REACH)) + (0.5 * sums[0.5] + 0.25 * sums[0.25])
            value = lax.rsqrt(jnp.where(here > 0.0, diagonal, 1.0))
            root[tile, at : at + count, :] = value
            roots.append(value)
        span = pl.ds(at, count)
        root_e[0, span, :], root_e[1, span, :] = shift_pair(roots[0], roots[1], 1)
        root_w[0, span, :], root_w[1, span, :] = shift_pair(roots[0], roots[1], -1)
    shifted_root = {0: root, 1: root_e, -1: root_w}
    for at, count in chunks_of(low, high, CHUNK):
        for tile in (0, 1):
            for b in (-1, 0, 1):
                goal_depth = shifted_depth[-b][tile, at : at + count, :]
                goal_root = shifted_root[-b][tile, at : at + count, :]
                goal_wet = goal_depth > 0.0
                for a in (-1, 0, 1):
                    if (a, b) == (0, 0):
                        continue
                    from_depth = depth[tile, at + a : at + a + count, :]
                    from_root = root[tile, at + a : at + a + count, :]
                    link = jnp.where(
                        jnp.minimum(goal_depth, from_depth) > 0.0, goal_depth + from_depth, 0.0
                    )
                    weights[SLOT[(a, b)], tile, at : at + count, :] = (
                        goal_root * (-2.0 * halves((a, b)))
                    ) * (link * from_root)

    dot_sums = {}

    def add_dot(key, left, right):
        product = left * right
        for r in range(0, product.shape[0], 8):
            piece = product[r : r + 8, :]
            dot_sums[key] = piece if key not in dot_sums else dot_sums[key] + piece

    row_chunks = [(low, 8)] + chunks_of(first, last, CHUNK) + [(last, 8)]
    for at, count in chunks_of(first, last, CHUNK):
        p0 = basis[0, at : at + count, :]
        r0 = basis[STEPS + 1, at : at + count, :]
        add_dot(("p", "p", 0), p0, p0)
        add_dot(("r", "r", 0), r0, r0)
        add_dot(("p", "r", 0), p0, r0)

    for power in range(1, STEPS + 1):
        chains = [("p", 0, power == STEPS)]
        if power < STEPS:
            chains.append(("r", STEPS + 1, power == STEPS - 1))
        for at, count in row_chunks:
            inner = first <= at < last
            fresh = {}
            held = {}
            factors = [
                {ab: weights[SLOT[ab], tile, at : at + count, :] for ab in DIRECTIONS}
                for tile in (0, 1)
            ]
            for name, origin, only_block in chains:
                if only_block and not inner:
                    continue
                slot = origin + power
                parts = []
                for tile, fields in ((0, basis), (1, basis_halo)):
                    taken = {
                        a: fields[slot - 1, at + a : at + a + count, :] for a in (-1, 0, 1)
                    }
                    if tile == 0:
                        held[name] = taken[0]
                    columns = {}
                    for b in (-1, 0, 1):
                        total = None
                        for a in (-1, 0, 1):
                            if (a, b) == (0, 0):
                                continue
                            term = factors[tile][(a, b)] * taken[a]
                            total = term if total is None else total + term
                        columns[b] = total
                    parts.append(columns)
                ahead = shift_pair(parts[0][1], parts[1][1], 1)
                behind = shift_pair(parts[0][-1], parts[1][-1], -1)
                for tile, fields in ((0, basis), (1, basis_halo)):
                    if tile == 1 and only_block:
                        continue
                    value = parts[tile][0] + ahead[tile] + behind[tile]
                    if power == 1:
                        value = 0.5 * value
                    else:
                        value = value - fields[slot - 2, at : at + count, :]
                    fields[slot, at : at + count, :] = value
                    if tile == 0:
                        fresh[name] = value
            if not inner:
                continue
            for name, _, _ in chains:
                add_dot((name, name, 2 * power), fresh[name], fresh[name])
                add_dot((name, name, 2 * power - 1), fresh[name], held[name])
            if power < STEPS:
                add_dot(("p", "r", 2 * power), fresh["p"], fresh["r"])
                add_dot(("p", "r", 2 * power - 1), fresh["p"], held["r"])
            else:
                add_dot(
                    ("p", "r", 2 * power - 1),
                    fresh["p"],
                    basis[STEPS + power, at : at + count, :],
                )
        for key in [key for key in dot_sums]:
            dots[order_of()[key]] = dot_sums.pop(key)

    number = len(order_of())
    pending = []
    lane = lax.broadcasted_iota(jnp.int32, (8, width), 1)
    home = lane - lax.broadcasted_iota(jnp.int32, (8, width), 0)
    message = jnp.zeros((8, width), jnp.float32)
    for g in range(number // 8):
        grouped = fold_sublanes([dots[8 * g + s] for s in range(8)])
        message = jnp.where(home == 8 * g, jnp.sum(grouped, axis=1, keepdims=True), message)
    message = jnp.sum(message, axis=0, keepdims=True)
    if direct:
        me = lat * n_lon + lon
        sums_all[me] = message
        copies = [
            pltpu.make_async_remote_copy(
                src_ref=sums_all.at[me], dst_ref=sums_all.at[me], send_sem=all_send.at[index],
                recv_sem=all_recv.at[index],
                device_id=(lax.rem(lat + a, n_lat), lax.rem(lon + b, n_lon)),
                device_id_type=MESH,
            )
            for index, (a, b) in enumerate(everyone)
        ]
        rounds = ((sums_all, n_lat * n_lon, copies),)
    else:
        rounds = (
            (sums_lat, n_lat, None, lat, True, lat_send, lat_recv),
            (sums_lon, n_lon, None, lon, False, lon_send, lon_recv),
        )
    for slots, size, copies, *rest in rounds:
        if copies is None:
            me, along_lat, send_sem, recv_sem = rest
            slots[me] = message
            copies = spread(slots.at[me], slots, send_sem, recv_sem, along_lat)
        for copy in copies:
            copy.start()
        for copy in copies:
            copy.wait_recv()
        terms = [slots[index] for index in range(size)]
        while len(terms) > 1:
            odd = terms[len(terms) // 2 * 2 :]
            terms = [x + y for x, y in zip(terms[0::2], terms[1::2])] + odd
        message = terms[0]
        pending.extend(copies)
    message = jnp.broadcast_to(message, (8, width))
    for g in range(number // 8):
        picked = jnp.sum(jnp.where(home == 8 * g, message, 0.0), axis=1, keepdims=True)
        moment_rows[8 * g : 8 * g + 8, :] = jnp.broadcast_to(picked, (8, width))
    moments = {}
    for kind in (("p", "p"), ("p", "r"), ("r", "r")):
        series = []
        for index in range(17 if kind == ("p", "p") else 16 if kind == ("p", "r") else 15):
            spot = order_of()[kind + (index,)]
            value = jnp.broadcast_to(moment_rows[spot : spot + 1, :], (8, width))
            series.append(value if index < 2 else 2.0 * value - series[index % 2])
        moments[kind] = series
    height_coords, residual_coords = coordinates(moments)
    for at in range(0, rows, 8):
        for coords, out in ((height_coords, out_height), (residual_coords, out_residual)):
            total = None
            for (chain, power), factor in sorted(coords.items(), key=lambda item: item[0]):
                slot = power + (0 if chain == "p" else STEPS + 1)
                term = factor * basis[slot, PAD + at : PAD + at + 8, :]
                total = term if total is None else total + term
            out[at : at + 8, :] = total

    for copy in pending:
        copy.wait_send()
    to_east.wait_send()
    to_west.wait_send()

    @pl.when(has_north)
    def _():
        for copy in northward:
            copy.wait_send()

    @pl.when(has_south)
    def _():
        for copy in southward:
            copy.wait_send()

    @pl.when(lat == top)
    def _():
        for copy in across:
            copy.wait_send()


@functools.cache
def order_of():
    keys = [("p", "p", k) for k in range(2 * STEPS + 1)]
    keys += [("p", "r", k) for k in range(2 * STEPS)]
    keys += [("r", "r", k) for k in range(2 * STEPS - 1)]
    return {key: index for index, key in enumerate(keys)}


def hand_over(height, residual, out_height, out_residual):
    out_height[...] = height[...]
    out_residual[...] = residual[...]


def per_device(n_lat, n_lon, forcing, search_direction, ocean_depth, land_mask, fold_map):
    rows, width = forcing.shape
    tall = rows + 2 * PAD
    f32 = jnp.float32
    own = pltpu.VMEM((rows, width), f32)
    pair = pltpu.VMEM((2, tall, width), f32)
    edge = pltpu.VMEM((32, width), f32)
    group_rows = rows * GROUP // width
    strip = pltpu.VMEM((group_rows, width), f32)
    everyone = n_lat * n_lon if n_lat * n_lon <= DIRECT_LIMIT else 2
    dma = pltpu.SemaphoreType.DMA
    block = pl.BlockSpec(memory_space=pltpu.VMEM)
    outs = pl.pallas_call(
        functools.partial(kernel, n_lat, n_lon),
        out_shape=[pltpu.VMEM((rows, width), f32)] * 2,
        in_specs=[pl.BlockSpec(memory_space=pl.ANY)] * 5,
        out_specs=[block] * 2,
        scratch_shapes=[
            own, own, own, pltpu.VMEM((rows, width), jnp.int32),
            pltpu.SMEM(fold_map.shape, jnp.int32),
            pair, pair, pair, pair, pair, pair,
            pltpu.VMEM((8, 2, tall, width), f32),
            pltpu.VMEM((2 * STEPS + 1, tall, width), f32),
            pltpu.VMEM((2 * STEPS + 1, tall, width), f32),
            edge, edge, edge,
            pltpu.VMEM((2, group_rows, width), f32),
            edge, edge, strip, strip,
            pltpu.VMEM((4, 16, width), f32),
            pltpu.VMEM((n_lon, 32, width), f32),
            pltpu.VMEM((6 * STEPS, 8, width), f32),
            pltpu.VMEM((n_lat, 1, width), f32),
            pltpu.VMEM((n_lon, 1, width), f32),
            pltpu.VMEM((everyone, 1, width), f32),
            pltpu.VMEM((6 * STEPS, width), f32),
            dma((5,)),
            dma((8,)), dma((8,)),
            dma((n_lon - 1,)), dma((n_lon - 1,)),
            dma((n_lat - 1,)), dma((n_lat - 1,)),
            dma((n_lon - 1,)), dma((n_lon - 1,)),
            dma((everyone - 1,)), dma((everyone - 1,)),
        ],
        compiler_params=pltpu.CompilerParams(collective_id=0, has_side_effects=True),
        name="tripole_cg",
    )(forcing, search_direction, ocean_depth, land_mask, fold_map)
    return pl.pallas_call(
        hand_over,
        out_shape=[jax.ShapeDtypeStruct((rows, width), f32)] * 2,
        in_specs=[block] * 2,
        out_specs=[block] * 2,
        name="hand_over",
    )(*(pltpu.with_memory_space_constraint(out, pltpu.VMEM) for out in outs))


def solution(mesh):
    cells = P("lat", "lon")
    return jax.shard_map(
        functools.partial(per_device, mesh.shape["lat"], mesh.shape["lon"]),
        mesh=mesh,
        in_specs=(cells, cells, cells, cells, P()),
        out_specs=(cells, cells),
        check_vma=False,
    )
```

profile of v0, /device:TPU:0, one launch (start us, length us, event | category | flops | bytes accessed | tf_op | source)
XLA Modules:
  0.0 22.6 jit_solution(16677264297971211782)
XLA Ops:
  0.6 21.3 %tripole_cg.1 = (f32[160,128]{1,0:T(8,128)S(1)}, f32[160,128]{1,0:T(8,128)S(1)}) custom-call(f32[160,128]{1,0:T(8,128)} %forcing_hbm.1, f32[160,128]{1,0:T(8,128)} %search_hbm.1, f32[160,128]{1,0:T(8,128)} %depth_hbm.1, s32[160,128]{1,0:T(8,128)} %mask_hbm.1, s32[1024]{0:T(1024)} %fold_hbm.1), custom_call_target="tpu_custom_call" | custom-call | tf_op jit(solution)/shard_map/tripole_cg/pallas_call | solution.py:585
  22.0 0.7 %hand_over.1 = (f32[160,128]{1,0:T(8,128)}, f32[160,128]{1,0:T(8,128)}) custom-call(f32[160,128]{1,0:T(8,128)S(1)} %get-tuple-element.4.height, f32[160,128]{1,0:T(8,128)S(1)} %get-tuple-element.5.residual), custom_call_target="tpu_custom_call" | custom-call | tf_op jit(solution)/shard_map/hand_over/pallas_call | solution.py:617
where the time goes:
time: 22.8 us; the launch traced here: 22.6 us
  Pallas kernels  22 us (96%)
  between operations  0.64 us (3%)
    pallas_call x1, Pallas kernels, per_device(): pl.pallas_call(functools.partial(kernel, n_lat, n_lon), out_shape=[pltpu....  21.3 us
    pallas_call x1, Pallas kernels, per_device(): pl.pallas_call(hand_over, out_shape=[jax.ShapeDtypeStruct((rows, width),...  0.68 us

commit v1 on v0

--- a/solution.py
+++ b/solution.py
@@ -132,12 +132,10 @@
 
 def kernel(
     n_lat, n_lon, forcing_hbm, search_hbm, depth_hbm, mask_hbm, fold_hbm,
-    out_height, out_residual, forcing, search, depth_in, mask_in, fold_map,
+    out_height, out_residual, loaded, mask_in, fold_map,
     depth, depth_e, depth_w, root, root_e, root_w, weights, basis, basis_halo,
-    row_north, row_south, fold_rows, packed, got_north, got_south, got_east, got_west,
-    corners, fold_all, dots, sums_lat, sums_lon, sums_all, moment_rows, load_sem,
-    near_send, near_recv, fold_send, fold_recv, lat_send, lat_recv, lon_send, lon_recv,
-    all_send, all_recv,
+    row_north, row_south, fold_rows, packed, got_rows, got_sides,
+    fold_all, dots, moment_rows, load_sem, near_send, near_recv, *moment_refs,
 ):
     rows, width = forcing_hbm.shape
     lat, lon = lax.axis_index("lat"), lax.axis_index("lon")
@@ -153,15 +151,12 @@
     def greet(place):
         pl.semaphore_signal(barrier, inc=1, device_id=place, device_id_type=MESH)
 
-    loads = [
-        pltpu.make_async_copy(source, target, load_sem.at[index])
-        for index, (source, target) in enumerate(
-            ((mask_hbm, mask_in), (depth_hbm, depth_in), (search_hbm, search),
-             (forcing_hbm, forcing), (fold_hbm, fold_map))
-        )
-    ]
-    for load in loads:
-        load.start()
+    for source, target, index in (
+        (mask_hbm, mask_in, 0), (depth_hbm, loaded.at[0], 1), (search_hbm, loaded.at[1], 1),
+        (forcing_hbm, loaded.at[2], 1), (fold_hbm, fold_map, 2),
+    ):
+        pltpu.make_async_copy(source, target, load_sem.at[index]).start()
+    depth_in, search, forcing = loaded.at[0], loaded.at[1], loaded.at[2]
     direct = n_lat * n_lon <= DIRECT_LIMIT
     everyone = [(a, b) for a in range(n_lat) for b in range(n_lon) if a or b]
     everyone.sort(key=lambda d: -min(d[0], n_lat - d[0]) - min(d[1], n_lon - d[1]))
@@ -178,8 +173,9 @@
             greet(place)
         greeted = n_lat - 1 + n_lon - 1 + 4
 
-    for load in loads:
-        load.wait()
+    pltpu.make_async_copy(mask_hbm, mask_in, load_sem.at[0]).wait()
+    pltpu.make_async_copy(loaded, loaded, load_sem.at[1]).wait()
+    pltpu.make_async_copy(fold_hbm, fold_map, load_sem.at[2]).wait()
     lane_group = lax.broadcasted_iota(jnp.int32, (group_rows, width), 1)
     west_edge = east_edge = None
     for g in range(n_groups):
@@ -234,15 +230,28 @@
 
     tail = pl.ds(group_rows - 16, 16)
     head = pl.ds(0, 16)
-    to_north = near(0, row_north, got_south, (north, lon))
-    to_south = near(1, row_south, got_north, (south, lon))
+    got_south, got_north = got_rows.at[0, 0:32], got_rows.at[1, 0:32]
+    got_west, got_east = got_sides.at[0], got_sides.at[1]
+    corners = [got_rows.at[index // 2, pl.ds(32 + 16 * (index % 2), 16)] for index in range(4)]
+    northward = (
+        near(0, row_north, got_south, (north, lon)),
+        near(0, packed.at[1, tail], corners[0], (north, east)),
+        near(0, packed.at[0, tail], corners[1], (north, west)),
+    )
+    southward = (
+        near(1, row_south, got_north, (south, lon)),
+        near(1, packed.at[1, head], corners[2], (south, east)),
+        near(1, packed.at[0, head], corners[3], (south, west)),
+    )
     to_east = near(2, packed.at[1], got_west, (lat, east))
-    to_west = near(3, packed.at[0], got_east, (lat, west))
-    to_ne = near(4, packed.at[1, tail], corners.at[0], (north, east))
-    to_nw = near(5, packed.at[0, tail], corners.at[1], (north, west))
-    to_se = near(6, packed.at[1, head], corners.at[2], (south, east))
-    to_sw = near(7, packed.at[0, head], corners.at[3], (south, west))
-    northward, southward = (to_north, to_ne, to_nw), (to_south, to_se, to_sw)
+    to_west = near(2, packed.at[0], got_east, (lat, west))
+
+    def arrival(index, block):
+        return near(index, block, block, (lat, lon))
+
+    from_south, from_north = arrival(0, got_rows.at[0]), arrival(1, got_rows.at[1])
+    from_sides = arrival(2, got_sides)
+    from_fold = arrival(3, fold_all.at[0 : n_lon - 1])
 
     def spread(source, slots, send_sem, recv_sem, along_lat):
         size = n_lat if along_lat else n_lon
@@ -252,15 +261,15 @@
             peer = lax.rem(me + d, size)
             copies.append(
                 pltpu.make_async_remote_copy(
-                    src_ref=source, dst_ref=slots.at[me], send_sem=send_sem.at[d - 1],
-                    recv_sem=recv_sem.at[d - 1],
+                    src_ref=source, dst_ref=slots.at[me], send_sem=send_sem,
+                    recv_sem=recv_sem,
                     device_id=(peer, lon) if along_lat else (lat, peer),
                     device_id_type=MESH,
                 )
             )
         return copies
 
-    across = spread(fold_rows, fold_all, fold_send, fold_recv, False)
+    across = spread(fold_rows, fold_all, near_send.at[3], near_recv.at[3], False)
 
     @pl.when(lat == top)
     def _():
@@ -293,19 +302,17 @@
                 jnp.where(lane >= width - cells, from_west, jnp.zeros_like(got_e)),
             )
 
-    to_east.wait_recv()
-    to_west.wait_recv()
+    from_sides.wait_recv()
     for g in range(n_groups):
         unpack(got_east[...], got_west[...], PAD + g * group_rows, g, group_rows)
 
     @pl.when(has_south)
     def _():
-        for copy in northward:
-            copy.wait_recv()
+        from_south.wait_recv()
         depth[0, 0:16, :] = got_south[0:16, :]
         basis[0, 8:16, :] = got_south[16:24, :]
         basis[STEPS + 1, 8:16, :] = got_south[24:32, :]
-        unpack(corners[1], corners[0], 0, n_groups - 1, 16)
+        unpack(corners[1][...], corners[0][...], 0, n_groups - 1, 16)
 
     @pl.when(lat == 0)
     def _():
@@ -318,17 +325,15 @@
 
     @pl.when(has_north)
     def _():
-        for copy in southward:
-            copy.wait_recv()
+        from_north.wait_recv()
         depth[0, last : last + 16, :] = got_north[0:16, :]
         basis[0, last : last + 8, :] = got_north[16:24, :]
         basis[STEPS + 1, last : last + 8, :] = got_north[24:32, :]
-        unpack(corners[3], corners[2], last, 0, 16)
+        unpack(corners[3][...], corners[2][...], last, 0, 16)
 
     @pl.when(lat == top)
     def _():
-        for copy in across:
-            copy.wait_recv()
+        from_fold.wait_recv()
         total = n_lon * width
         pivot = lax.rem(fold_map[0] - lon * width + total, total)
         block, offset = pivot // width, lax.rem(pivot, width)
@@ -482,38 +487,44 @@
         message = jnp.where(home == 8 * g, jnp.sum(grouped, axis=1, keepdims=True), message)
     message = jnp.sum(message, axis=0, keepdims=True)
     if direct:
+        slots, send_sem, recv_sem = moment_refs
         me = lat * n_lon + lon
-        sums_all[me] = message
+        slots[me] = message
         copies = [
             pltpu.make_async_remote_copy(
-                src_ref=sums_all.at[me], dst_ref=sums_all.at[me], send_sem=all_send.at[index],
-                recv_sem=all_recv.at[index],
+                src_ref=slots.at[me], dst_ref=slots.at[me], send_sem=send_sem,
+                recv_sem=recv_sem,
                 device_id=(lax.rem(lat + a, n_lat), lax.rem(lon + b, n_lon)),
                 device_id_type=MESH,
             )
-            for index, (a, b) in enumerate(everyone)
+            for a, b in everyone
         ]
-        rounds = ((sums_all, n_lat * n_lon, copies),)
+        rounds = ((slots, n_lat * n_lon, copies, send_sem, recv_sem),)
     else:
+        slots_lat, slots_lon, lat_send, lat_recv, lon_send, lon_recv = moment_refs
         rounds = (
-            (sums_lat, n_lat, None, lat, True, lat_send, lat_recv),
-            (sums_lon, n_lon, None, lon, False, lon_send, lon_recv),
+            (slots_lat, n_lat, None, lat_send, lat_recv, lat, True),
+            (slots_lon, n_lon, None, lon_send, lon_recv, lon, False),
         )
-    for slots, size, copies, *rest in rounds:
+    for slots, size, copies, send_sem, recv_sem, *rest in rounds:
         if copies is None:
-            me, along_lat, send_sem, recv_sem = rest
+            me, along_lat = rest
             slots[me] = message
             copies = spread(slots.at[me], slots, send_sem, recv_sem, along_lat)
         for copy in copies:
             copy.start()
-        for copy in copies:
-            copy.wait_recv()
+        others = slots.at[0 : size - 1]
+        whole = pltpu.make_async_remote_copy(
+            src_ref=others, dst_ref=others, send_sem=send_sem, recv_sem=recv_sem,
+            device_id=(lat, lon), device_id_type=MESH,
+        )
+        whole.wait_recv()
         terms = [slots[index] for index in range(size)]
         while len(terms) > 1:
             odd = terms[len(terms) // 2 * 2 :]
             terms = [x + y for x, y in zip(terms[0::2], terms[1::2])] + odd
         message = terms[0]
-        pending.extend(copies)
+        pending.append(whole)
     message = jnp.broadcast_to(message, (8, width))
     for g in range(number // 8):
         picked = jnp.sum(jnp.where(home == 8 * g, message, 0.0), axis=1, keepdims=True)
@@ -538,23 +549,19 @@
 
     for copy in pending:
         copy.wait_send()
-    to_east.wait_send()
-    to_west.wait_send()
+    from_sides.wait_send()
 
     @pl.when(has_north)
     def _():
-        for copy in northward:
-            copy.wait_send()
+        from_south.wait_send()
 
     @pl.when(has_south)
     def _():
-        for copy in southward:
-            copy.wait_send()
+        from_north.wait_send()
 
     @pl.when(lat == top)
     def _():
-        for copy in across:
-            copy.wait_send()
+        from_fold.wait_send()
 
 
 @functools.cache
@@ -574,13 +581,14 @@
     rows, width = forcing.shape
     tall = rows + 2 * PAD
     f32 = jnp.float32
-    own = pltpu.VMEM((rows, width), f32)
     pair = pltpu.VMEM((2, tall, width), f32)
     edge = pltpu.VMEM((32, width), f32)
     group_rows = rows * GROUP // width
-    strip = pltpu.VMEM((group_rows, width), f32)
-    everyone = n_lat * n_lon if n_lat * n_lon <= DIRECT_LIMIT else 2
     dma = pltpu.SemaphoreType.DMA
+    if n_lat * n_lon <= DIRECT_LIMIT:
+        moment_refs = [pltpu.VMEM((n_lat * n_lon, 1, width), f32), dma, dma]
+    else:
+        moment_refs = [pltpu.VMEM((size, 1, width), f32) for size in (n_lat, n_lon)] + [dma] * 4
     block = pl.BlockSpec(memory_space=pltpu.VMEM)
     outs = pl.pallas_call(
         functools.partial(kernel, n_lat, n_lon),
@@ -588,7 +596,7 @@
         in_specs=[pl.BlockSpec(memory_space=pl.ANY)] * 5,
         out_specs=[block] * 2,
         scratch_shapes=[
-            own, own, own, pltpu.VMEM((rows, width), jnp.int32),
+            pltpu.VMEM((3, rows, width), f32), pltpu.VMEM((rows, width), jnp.int32),
             pltpu.SMEM(fold_map.shape, jnp.int32),
             pair, pair, pair, pair, pair, pair,
             pltpu.VMEM((8, 2, tall, width), f32),
@@ -596,20 +604,13 @@
             pltpu.VMEM((2 * STEPS + 1, tall, width), f32),
             edge, edge, edge,
             pltpu.VMEM((2, group_rows, width), f32),
-            edge, edge, strip, strip,
-            pltpu.VMEM((4, 16, width), f32),
+            pltpu.VMEM((2, 64, width), f32),
+            pltpu.VMEM((2, group_rows, width), f32),
             pltpu.VMEM((n_lon, 32, width), f32),
             pltpu.VMEM((6 * STEPS, 8, width), f32),
-            pltpu.VMEM((n_lat, 1, width), f32),
-            pltpu.VMEM((n_lon, 1, width), f32),
-            pltpu.VMEM((everyone, 1, width), f32),
             pltpu.VMEM((6 * STEPS, width), f32),
-            dma((5,)),
-            dma((8,)), dma((8,)),
-            dma((n_lon - 1,)), dma((n_lon - 1,)),
-            dma((n_lat - 1,)), dma((n_lat - 1,)),
-            dma((n_lon - 1,)), dma((n_lon - 1,)),
-            dma((everyone - 1,)), dma((everyone - 1,)),
+            dma((3,)), dma((4,)), dma((4,)),
+            *moment_refs,
         ],
         compiler_params=pltpu.CompilerParams(collective_id=0, has_side_effects=True),
         name="tripole_cg",

time: 22.8 us -> 21.8 us (0.956)
  Pallas kernels: 22 us -> 21 us
    pallas_call x1, Pallas kernels: 21.3 us -> 20.3 us  [per_device(): pl.pallas_call(functools.partial(kernel, n_lat, n_lon), out_shape=[pltpu....]
where the time goes in v1:
time: 21.8 us; the launch traced here: 21.6 us
  Pallas kernels  21 us (96%)
  between operations  0.64 us (3%)
    pallas_call x1, Pallas kernels, per_device(): pl.pallas_call(functools.partial(kernel, n_lat, n_lon), out_shape=[pltpu....  20.3 us
    pallas_call x1, Pallas kernels, per_device(): pl.pallas_call(hand_over, out_shape=[jax.ShapeDtypeStruct((rows, width),...  0.68 us

profile of v1, /device:TPU:0, one launch (start us, length us, event | category | flops | bytes accessed | tf_op | source)
XLA Modules:
  0.0 21.6 jit_solution(7044936770878279530)
XLA Ops:
  0.6 20.3 %tripole_cg.1 = (f32[160,128]{1,0:T(8,128)S(1)}, f32[160,128]{1,0:T(8,128)S(1)}) custom-call(f32[160,128]{1,0:T(8,128)} %forcing_hbm.1, f32[160,128]{1,0:T(8,128)} %search_hbm.1, f32[160,128]{1,0:T(8,128)} %depth_hbm.1, s32[160,128]{1,0:T(8,128)} %mask_hbm.1, s32[1024]{0:T(1024)} %fold_hbm.1), custom_call_target="tpu_custom_call" | custom-call | tf_op jit(solution)/shard_map/tripole_cg/pallas_call | solution.py:593
  21.0 0.7 %hand_over.1 = (f32[160,128]{1,0:T(8,128)}, f32[160,128]{1,0:T(8,128)}) custom-call(f32[160,128]{1,0:T(8,128)S(1)} %get-tuple-element.4.height, f32[160,128]{1,0:T(8,128)S(1)} %get-tuple-element.5.residual), custom_call_target="tpu_custom_call" | custom-call | tf_op jit(solution)/shard_map/hand_over/pallas_call | solution.py:618

commit v2 on v1

--- a/solution.py
+++ b/solution.py
@@ -13,6 +13,9 @@
 PAD = 16
 GROUP = 32
 CHUNK = 16
+LIP = STEPS + 1
+MARGIN = 12
+BAND = 32
 DIRECT_LIMIT = 64
 
 DIRECTIONS = ((1, 0), (-1, 0), (0, 1), (0, -1), (1, 1), (-1, -1), (1, -1), (-1, 1))
@@ -25,17 +28,6 @@
 
 def chunks_of(low, high, size):
     return [(at, min(size, high - at)) for at in range(low, high, size)]
-
-
-def shift_pair(centre, halo, step):
-    width = centre.shape[1]
-    lane = lax.broadcasted_iota(jnp.int32, centre.shape, 1)
-    edge = lane == (0 if step == 1 else width - 1)
-    turn = width - 1 if step == 1 else 1
-    return (
-        pltpu.roll(jnp.where(edge, halo, centre), turn, 1),
-        pltpu.roll(jnp.where(edge, centre, halo), turn, 1),
-    )
 
 
 def turned(x, shift):
@@ -130,11 +122,141 @@
     return parts[0]
 
 
+def kept(at, count, regions):
+    row = lax.broadcasted_iota(jnp.int32, (8, regions[0][2].shape[1]), 0)
+    masks = []
+    for r in range(at, at + count, 8):
+        mask = None
+        for low, high, lanes in regions:
+            if low >= r + 8 or high <= r:
+                continue
+            part = lanes
+            if low > r or high < r + 8:
+                part = lanes & (row >= low - r) & (row < high - r)
+            mask = part if mask is None else mask | part
+        masks.append(mask)
+    return masks
+
+
+def prepare(rows, depth_root, shifted, weights, basis):
+    width = depth_root.shape[2]
+    zero = jnp.zeros((8, width), jnp.float32)
+    for at in (0, 8 + rows):
+        span = pl.ds(at, 8)
+        depth_root[0, span, :] = zero
+        depth_root[1, span, :] = zero
+        for slot in range(2 * STEPS + 1):
+            if slot not in (STEPS, 2 * STEPS):
+                basis[slot, span, :] = zero
+
+    depth, root = depth_root.at[0], depth_root.at[1]
+    for at, count in chunks_of(0, rows + 16, CHUNK):
+        span = pl.ds(at, count)
+        shifted[0, span, :] = turned(depth[span, :], -1)
+        shifted[1, span, :] = turned(depth[span, :], 1)
+    shifted_depth = {0: depth, 1: shifted.at[0], -1: shifted.at[1]}
+    for at, count in chunks_of(8, 8 + rows, CHUNK):
+        here = depth[at : at + count, :]
+        sums = {0.5: None, 0.25: None}
+        for a, b in DIRECTIONS:
+            beside = shifted_depth[b][at + a : at + a + count, :]
+            link = jnp.where(beside > 0.0, here + beside, 0.0)
+            factor = halves((a, b))
+            sums[factor] = link if sums[factor] is None else sums[factor] + link
+        diagonal = here * (1.0 / (REACH * REACH)) + (0.5 * sums[0.5] + 0.25 * sums[0.25])
+        value = lax.rsqrt(jnp.where(here > 0.0, diagonal, 1.0))
+        span = pl.ds(at, count)
+        root[span, :] = value
+        shifted[2, span, :] = turned(value, -1)
+        shifted[3, span, :] = turned(value, 1)
+    shifted_root = {0: root, 1: shifted.at[2], -1: shifted.at[3]}
+    for at, count in chunks_of(8, 8 + rows, CHUNK):
+        for b in (-1, 0, 1):
+            goal_depth = shifted_depth[-b][at : at + count, :]
+            goal_root = shifted_root[-b][at : at + count, :]
+            for a in (-1, 0, 1):
+                if (a, b) == (0, 0):
+                    continue
+                from_depth = depth[at + a : at + a + count, :]
+                from_root = root[at + a : at + a + count, :]
+                link = jnp.where(
+                    jnp.minimum(goal_depth, from_depth) > 0.0, goal_depth + from_depth, 0.0
+                )
+                weights[SLOT[(a, b)], at : at + count, :] = (
+                    goal_root * (-2.0 * halves((a, b)))
+                ) * (link * from_root)
+
+
+def march(rows, weights, basis, keep, add_dot, flush, new):
+    def masked(masks, value):
+        return [
+            None if mask is None else jnp.where(mask, value[8 * i : 8 * i + 8, :], 0.0)
+            for i, mask in enumerate(masks)
+        ]
+
+    def dot(key, left, right):
+        for i, piece in enumerate(left):
+            if piece is not None:
+                add_dot(key, piece, right[8 * i : 8 * i + 8, :])
+
+    row_chunks = chunks_of(8, 8 + rows, CHUNK)
+    for at, count in row_chunks:
+        p0 = basis[0, at : at + count, :]
+        r0 = basis[STEPS + 1, at : at + count, :]
+        masks = keep(at - 8, count)
+        p0_kept, r0_kept = masked(masks, p0), masked(masks, r0)
+        dot(("p", "p", 0), p0_kept, p0)
+        dot(("r", "r", 0), r0_kept, r0)
+        dot(("p", "r", 0), p0_kept, r0)
+
+    for power in range(1, STEPS + 1):
+        chains = [("p", 0)] + ([("r", STEPS + 1)] if power < STEPS else [])
+        for at, count in row_chunks:
+            fresh = {}
+            held = {}
+            factors = {ab: weights[SLOT[ab], at : at + count, :] for ab in DIRECTIONS}
+            for name, origin in chains:
+                slot = origin + power
+                taken = {a: basis[slot - 1, at + a : at + a + count, :] for a in (-1, 0, 1)}
+                held[name] = taken[0]
+                columns = {}
+                for b in (-1, 0, 1):
+                    total = None
+                    for a in (-1, 0, 1):
+                        if (a, b) == (0, 0):
+                            continue
+                        term = factors[(a, b)] * taken[a]
+                        total = term if total is None else total + term
+                    columns[b] = total
+                value = columns[0] + turned(columns[1], -1) + turned(columns[-1], 1)
+                if power == 1:
+                    value = 0.5 * value
+                else:
+                    value = value - basis[slot - 2, at : at + count, :]
+                basis[slot, at : at + count, :] = value
+                fresh[name] = value
+            masks = keep(at - 8, count)
+            fresh_kept = {name: masked(masks, fresh[name]) for name, _ in chains}
+            for name, _ in chains:
+                dot((name, name, 2 * power), fresh_kept[name], fresh[name])
+                dot((name, name, 2 * power - 1), fresh_kept[name], held[name])
+            if power < STEPS:
+                dot(("p", "r", 2 * power), fresh_kept["p"], fresh["r"])
+                dot(("p", "r", 2 * power - 1), fresh_kept["p"], held["r"])
+            else:
+                dot(
+                    ("p", "r", 2 * power - 1),
+                    fresh_kept["p"],
+                    basis[STEPS + power, at : at + count, :],
+                )
+        flush(new)
+
+
 def kernel(
     n_lat, n_lon, forcing_hbm, search_hbm, depth_hbm, mask_hbm, fold_hbm,
     out_height, out_residual, loaded, mask_in, fold_map,
-    depth, depth_e, depth_w, root, root_e, root_w, weights, basis, basis_halo,
-    row_north, row_south, fold_rows, packed, got_rows, got_sides,
+    centre, side, wide, wide_shifted, wide_weights, wide_basis, seam, seam_shifted,
+    seam_weights, seam_basis, patch, row_north, row_south, fold_rows, packed, got_rows, got_sides,
     fold_all, dots, moment_rows, load_sem, near_send, near_recv, *moment_refs,
 ):
     rows, width = forcing_hbm.shape
@@ -159,7 +281,7 @@
     depth_in, search, forcing = loaded.at[0], loaded.at[1], loaded.at[2]
     direct = n_lat * n_lon <= DIRECT_LIMIT
     everyone = [(a, b) for a in range(n_lat) for b in range(n_lon) if a or b]
-    everyone.sort(key=lambda d: -min(d[0], n_lat - d[0]) - min(d[1], n_lon - d[1]))
+    everyone.sort(key=lambda d: (d[1] or n_lon, d[0] or n_lat))
     if direct:
         for a, b in everyone:
             greet((lax.rem(lat + a, n_lat), lax.rem(lon + b, n_lon)))
@@ -185,9 +307,12 @@
         deep = depth_in[here, :] * flag
         moving = search[here, :] * flag
         left = forcing[here, :] * flag
-        depth[0, there, :] = deep
-        basis[0, there, :] = moving
-        basis[STEPS + 1, there, :] = left
+        for index, value in enumerate((deep, moving, left)):
+            centre[index, there, :] = value
+        inner = pl.ds(8 + g * group_rows, group_rows)
+        wide[0, inner, :] = deep
+        wide_basis[0, inner, :] = moving
+        wide_basis[STEPS + 1, inner, :] = left
         inside = lane_group - g * GROUP
         to_west = jnp.where(
             inside < 9,
@@ -204,20 +329,16 @@
     packed[0] = west_edge
     packed[1] = east_edge
     first, last = PAD, PAD + rows
-    row_south[0:16, :] = depth[0, first : first + 16, :]
-    row_south[16:24, :] = basis[0, first : first + 8, :]
-    row_south[24:32, :] = basis[STEPS + 1, first : first + 8, :]
-    row_north[0:16, :] = depth[0, last - 16 : last, :]
-    row_north[16:24, :] = basis[0, last - 8 : last, :]
-    row_north[24:32, :] = basis[STEPS + 1, last - 8 : last, :]
+    spans = ((0, 0, 16), (1, 16, 8), (2, 24, 8))
+    for index, at, count in spans:
+        row_south[at : at + count, :] = centre[index, first : first + count, :]
+        row_north[at : at + count, :] = centre[index, last - count : last, :]
 
     @pl.when(lat == top)
     def _():
-        for r in range(16):
-            fold_rows[r : r + 1, :] = depth[0, last - 1 - r : last - r, :]
-        for r in range(8):
-            fold_rows[16 + r : 17 + r, :] = basis[0, last - 1 - r : last - r, :]
-            fold_rows[24 + r : 25 + r, :] = basis[STEPS + 1, last - 1 - r : last - r, :]
+        for index, at, count in spans:
+            for r in range(count):
+                fold_rows[at + r : at + r + 1, :] = centre[index, last - 1 - r : last - r, :]
         fold_all[lon] = fold_rows[...]
 
     pl.semaphore_wait(barrier, greeted)
@@ -289,19 +410,48 @@
         for copy in southward:
             copy.start()
 
+    dot_sums = {}
+
+    def add_dot(key, left, right):
+        product = left * right
+        for r in range(0, product.shape[0], 8):
+            piece = product[r : r + 8, :]
+            dot_sums[key] = piece if key not in dot_sums else dot_sums[key] + piece
+
+    def flush(new):
+        for key in list(dot_sums):
+            total = dot_sums.pop(key)
+            spot = order_of()[key]
+            dots[spot] = total if new else dots[spot] + total
+
+    lane8 = lax.broadcasted_iota(jnp.int32, (8, width), 1)
+    nothing = jnp.zeros((8, width), jnp.float32)
+
+    prepare(rows, wide, wide_shifted, wide_weights, wide_basis)
+    middle = (lane8 >= LIP) & (lane8 < width - LIP)
+
+    def keep_wide(at, count):
+        return kept(at, count, [(LIP, rows - LIP, middle)])
+
+    march(rows, wide_weights, wide_basis, keep_wide, add_dot, flush, True)
+
     def unpack(got_e, got_w, start, g, count):
         lane = lax.broadcasted_iota(jnp.int32, (count, width), 1)
         base = -g * GROUP
-        spans = ((0, 9, depth.at[1]), (9, 8, basis_halo.at[0]), (17, 8, basis_halo.at[STEPS + 1]))
-        for offset, cells, target in spans:
+        for index, offset, cells in ((0, 0, 9), (1, 9, 8), (2, 17, 8)):
             from_east = turned(got_e, base - offset)
             from_west = turned(got_w, base - offset - cells)
-            target[start : start + count, :] = jnp.where(
+            side[index, start : start + count, :] = jnp.where(
                 lane < cells,
                 from_east,
                 jnp.where(lane >= width - cells, from_west, jnp.zeros_like(got_e)),
             )
 
+    for index in (1, 2):
+        for at in (0, last + 8):
+            centre[index, at : at + 8, :] = nothing
+            side[index, at : at + 8, :] = nothing
+
     from_sides.wait_recv()
     for g in range(n_groups):
         unpack(got_east[...], got_west[...], PAD + g * group_rows, g, group_rows)
@@ -309,26 +459,23 @@
     @pl.when(has_south)
     def _():
         from_south.wait_recv()
-        depth[0, 0:16, :] = got_south[0:16, :]
-        basis[0, 8:16, :] = got_south[16:24, :]
-        basis[STEPS + 1, 8:16, :] = got_south[24:32, :]
+        centre[0, 0:16, :] = got_south[0:16, :]
+        centre[1, 8:16, :] = got_south[16:24, :]
+        centre[2, 8:16, :] = got_south[24:32, :]
         unpack(corners[1][...], corners[0][...], 0, n_groups - 1, 16)
 
     @pl.when(lat == 0)
     def _():
-        nothing = jnp.zeros((16, width), jnp.float32)
-        for target in (depth.at[0], depth.at[1]):
-            target[0:16, :] = nothing
-        for power in (0, STEPS + 1):
-            basis[power, 0:16, :] = nothing
-            basis_halo[power, 0:16, :] = nothing
+        for target in (centre, side):
+            for index, at in ((0, 0), (0, 8), (1, 8), (2, 8)):
+                target[index, at : at + 8, :] = nothing
 
     @pl.when(has_north)
     def _():
         from_north.wait_recv()
-        depth[0, last : last + 16, :] = got_north[0:16, :]
-        basis[0, last : last + 8, :] = got_north[16:24, :]
-        basis[STEPS + 1, last : last + 8, :] = got_north[24:32, :]
+        centre[0, last : last + 16, :] = got_north[0:16, :]
+        centre[1, last : last + 8, :] = got_north[16:24, :]
+        centre[2, last : last + 8, :] = got_north[24:32, :]
         unpack(corners[3][...], corners[2][...], last, 0, 16)
 
     @pl.when(lat == top)
@@ -346,136 +493,64 @@
 
         ahead, same, behind, beyond = (mirrored(which) for which in (1, 0, -1, -2))
         close = lane <= offset
-        centre = jnp.where(close, same, behind)
+        value = jnp.where(close, same, behind)
         halo = jnp.where(
             lane < width // 2, jnp.where(close, behind, beyond), jnp.where(close, ahead, same)
         )
-        for value, deep, fields in ((centre, depth.at[0], basis), (halo, depth.at[1], basis_halo)):
-            deep[last : last + 16, :] = value[0:16, :]
-            fields[0, last : last + 8, :] = value[16:24, :]
-            fields[STEPS + 1, last : last + 8, :] = value[24:32, :]
-
-    low, high = PAD - 8, last + 8
-    for at, count in chunks_of(0, rows + 2 * PAD, CHUNK):
-        span = pl.ds(at, count)
-        centre, halo = depth[0, span, :], depth[1, span, :]
-        depth_e[0, span, :], depth_e[1, span, :] = shift_pair(centre, halo, 1)
-        depth_w[0, span, :], depth_w[1, span, :] = shift_pair(centre, halo, -1)
-    shifted_depth = {0: depth, 1: depth_e, -1: depth_w}
-    for at, count in chunks_of(low, high, CHUNK):
-        roots = []
-        for tile in (0, 1):
-            here = depth[tile, at : at + count, :]
-            sums = {0.5: None, 0.25: None}
-            for a, b in DIRECTIONS:
-                beside = shifted_depth[b][tile, at + a : at + a + count, :]
-                link = jnp.where(beside > 0.0, here + beside, 0.0)
-                factor = halves((a, b))
-                sums[factor] = link if sums[factor] is None else sums[factor] + link
-            diagonal = here * (1.0 / (REACH * REACH)) + (0.5 * sums[0.5] + 0.25 * sums[0.25])
-            value = lax.rsqrt(jnp.where(here > 0.0, diagonal, 1.0))
-            root[tile, at : at + count, :] = value
-            roots.append(value)
-        span = pl.ds(at, count)
-        root_e[0, span, :], root_e[1, span, :] = shift_pair(roots[0], roots[1], 1)
-        root_w[0, span, :], root_w[1, span, :] = shift_pair(roots[0], roots[1], -1)
-    shifted_root = {0: root, 1: root_e, -1: root_w}
-    for at, count in chunks_of(low, high, CHUNK):
-        for tile in (0, 1):
-            for b in (-1, 0, 1):
-                goal_depth = shifted_depth[-b][tile, at : at + count, :]
-                goal_root = shifted_root[-b][tile, at : at + count, :]
-                goal_wet = goal_depth > 0.0
-                for a in (-1, 0, 1):
-                    if (a, b) == (0, 0):
-                        continue
-                    from_depth = depth[tile, at + a : at + a + count, :]
-                    from_root = root[tile, at + a : at + a + count, :]
-                    link = jnp.where(
-                        jnp.minimum(goal_depth, from_depth) > 0.0, goal_depth + from_depth, 0.0
-                    )
-                    weights[SLOT[(a, b)], tile, at : at + count, :] = (
-                        goal_root * (-2.0 * halves((a, b)))
-                    ) * (link * from_root)
-
-    dot_sums = {}
-
-    def add_dot(key, left, right):
-        product = left * right
-        for r in range(0, product.shape[0], 8):
-            piece = product[r : r + 8, :]
-            dot_sums[key] = piece if key not in dot_sums else dot_sums[key] + piece
-
-    row_chunks = [(low, 8)] + chunks_of(first, last, CHUNK) + [(last, 8)]
-    for at, count in chunks_of(first, last, CHUNK):
-        p0 = basis[0, at : at + count, :]
-        r0 = basis[STEPS + 1, at : at + count, :]
-        add_dot(("p", "p", 0), p0, p0)
-        add_dot(("r", "r", 0), r0, r0)
-        add_dot(("p", "r", 0), p0, r0)
-
-    for power in range(1, STEPS + 1):
-        chains = [("p", 0, power == STEPS)]
-        if power < STEPS:
-            chains.append(("r", STEPS + 1, power == STEPS - 1))
-        for at, count in row_chunks:
-            inner = first <= at < last
-            fresh = {}
-            held = {}
-            factors = [
-                {ab: weights[SLOT[ab], tile, at : at + count, :] for ab in DIRECTIONS}
-                for tile in (0, 1)
-            ]
-            for name, origin, only_block in chains:
-                if only_block and not inner:
-                    continue
-                slot = origin + power
-                parts = []
-                for tile, fields in ((0, basis), (1, basis_halo)):
-                    taken = {
-                        a: fields[slot - 1, at + a : at + a + count, :] for a in (-1, 0, 1)
-                    }
-                    if tile == 0:
-                        held[name] = taken[0]
-                    columns = {}
-                    for b in (-1, 0, 1):
-                        total = None
-                        for a in (-1, 0, 1):
-                            if (a, b) == (0, 0):
-                                continue
-                            term = factors[tile][(a, b)] * taken[a]
-                            total = term if total is None else total + term
-                        columns[b] = total
-                    parts.append(columns)
-                ahead = shift_pair(parts[0][1], parts[1][1], 1)
-                behind = shift_pair(parts[0][-1], parts[1][-1], -1)
-                for tile, fields in ((0, basis), (1, basis_halo)):
-                    if tile == 1 and only_block:
-                        continue
-                    value = parts[tile][0] + ahead[tile] + behind[tile]
-                    if power == 1:
-                        value = 0.5 * value
-                    else:
-                        value = value - fields[slot - 2, at : at + count, :]
-                    fields[slot, at : at + count, :] = value
-                    if tile == 0:
-                        fresh[name] = value
-            if not inner:
-                continue
-            for name, _, _ in chains:
-                add_dot((name, name, 2 * power), fresh[name], fresh[name])
-                add_dot((name, name, 2 * power - 1), fresh[name], held[name])
-            if power < STEPS:
-                add_dot(("p", "r", 2 * power), fresh["p"], fresh["r"])
-                add_dot(("p", "r", 2 * power - 1), fresh["p"], held["r"])
-            else:
-                add_dot(
-                    ("p", "r", 2 * power - 1),
-                    fresh["p"],
-                    basis[STEPS + power, at : at + count, :],
+        for source, target in ((value, centre), (halo, side)):
+            target[0, last : last + 16, :] = source[0:16, :]
+            target[1, last : last + 8, :] = source[16:24, :]
+            target[2, last : last + 8, :] = source[24:32, :]
+
+    n_parts = width // GROUP // 2
+    part_rows = rows // n_parts
+    strip_rows = part_rows + 2 * MARGIN
+    seam_rows = strip_rows + 2 * BAND
+    north_at, south_at = strip_rows, strip_rows + BAND
+    own = GROUP - LIP
+    targets = (seam.at[0], seam_basis.at[0], seam_basis.at[STEPS + 1])
+    for index, target in enumerate(targets):
+        for at in range(0, strip_rows, 8):
+            value = None
+            for q in range(n_parts):
+                span = slice(PAD + q * part_rows - MARGIN + at, PAD + q * part_rows - MARGIN + at + 8)
+                inside, outside = centre[index, span, :], side[index, span, :]
+                east_slot = turned(
+                    jnp.where(lane8 >= width - own, inside, outside), q * GROUP - (width - own)
                 )
-        for key in [key for key in dot_sums]:
-            dots[order_of()[key]] = dot_sums.pop(key)
+                west_slot = turned(
+                    jnp.where(lane8 < own, inside, outside), (n_parts + q) * GROUP + LIP
+                )
+                if q == 0:
+                    value = jnp.where(lane8 < n_parts * GROUP, east_slot, west_slot)
+                else:
+                    mixed = jnp.where(lane8 < n_parts * GROUP, east_slot, west_slot)
+                    value = jnp.where((lane8 // GROUP) % n_parts >= q, mixed, value)
+            target[8 + at : 16 + at, :] = value
+        for at in range(0, BAND, 8):
+            low = last + LIP - BAND + at
+            target[8 + north_at + at : 16 + north_at + at, :] = centre[index, low : low + 8, :]
+            low = first - LIP + at
+            target[8 + south_at + at : 16 + south_at + at, :] = centre[index, low : low + 8, :]
+
+    prepare(seam_rows, seam, seam_shifted, seam_weights, seam_basis)
+    slot_lane = lax.rem(lane8, GROUP)
+    east_half = lane8 < n_parts * GROUP
+    strip_lanes = jnp.where(east_half, slot_lane - (own - LIP), slot_lane - LIP)
+    strip_lanes = (strip_lanes >= 0) & (strip_lanes < LIP)
+
+    def keep_seam(at, count):
+        return kept(
+            at,
+            count,
+            [
+                (MARGIN, MARGIN + part_rows, strip_lanes),
+                (north_at + BAND - 2 * LIP, north_at + BAND - LIP, middle),
+                (south_at + LIP, south_at + 2 * LIP, middle),
+            ],
+        )
+
+    march(seam_rows, seam_weights, seam_basis, keep_seam, add_dot, flush, False)
 
     number = len(order_of())
     pending = []
@@ -538,14 +613,43 @@
             series.append(value if index < 2 else 2.0 * value - series[index % 2])
         moments[kind] = series
     height_coords, residual_coords = coordinates(moments)
+    wanted = (height_coords, residual_coords)
+
+    def combined(fields, at):
+        totals = [None, None]
+        for chain, power in sorted(height_coords | residual_coords):
+            slot = power + (0 if chain == "p" else STEPS + 1)
+            field = fields[slot, 8 + at : 16 + at, :]
+            for which, coords in enumerate(wanted):
+                if (chain, power) in coords:
+                    term = coords[(chain, power)] * field
+                    totals[which] = term if totals[which] is None else totals[which] + term
+        return totals
+
+    for at in range(0, seam_rows, 8):
+        for which, total in enumerate(combined(seam_basis, at)):
+            patch[which, at : at + 8, :] = total
+    row8 = lax.broadcasted_iota(jnp.int32, (8, width), 0)
     for at in range(0, rows, 8):
-        for coords, out in ((height_coords, out_height), (residual_coords, out_residual)):
-            total = None
-            for (chain, power), factor in sorted(coords.items(), key=lambda item: item[0]):
-                slot = power + (0 if chain == "p" else STEPS + 1)
-                term = factor * basis[slot, PAD + at : PAD + at + 8, :]
-                total = term if total is None else total + term
-            out[at : at + 8, :] = total
+        q = at // part_rows
+        for which, total in enumerate(combined(wide_basis, at)):
+            for low, high, source in (
+                (0, LIP, south_at + LIP),
+                (rows - LIP, rows, north_at + BAND - LIP - rows),
+            ):
+                if low < at + 8 and high > at:
+                    edge = patch[which, source + at : source + at + 8, :]
+                    if low <= at and high >= at + 8:
+                        total = edge
+                    else:
+                        total = jnp.where((row8 >= low - at) & (row8 < high - at), edge, total)
+            spot = at - q * part_rows + MARGIN
+            strip = patch[which, spot : spot + 8, :]
+            total = jnp.where(lane8 < LIP, turned(strip, -(n_parts + q) * GROUP - LIP), total)
+            total = jnp.where(
+                lane8 >= width - LIP, turned(strip, width - own - q * GROUP), total
+            )
+            (out_height, out_residual)[which][at : at + 8, :] = total
 
     for copy in pending:
         copy.wait_send()
@@ -581,7 +685,15 @@
     rows, width = forcing.shape
     tall = rows + 2 * PAD
     f32 = jnp.float32
-    pair = pltpu.VMEM((2, tall, width), f32)
+    n_parts = width // GROUP // 2
+    seam_rows = rows // n_parts + 2 * MARGIN + 2 * BAND
+
+    def tile(count):
+        return [
+            pltpu.VMEM((planes, count + 16, width), f32)
+            for planes in (2, 4, 8, 2 * STEPS + 1)
+        ]
+
     edge = pltpu.VMEM((32, width), f32)
     group_rows = rows * GROUP // width
     dma = pltpu.SemaphoreType.DMA
@@ -598,10 +710,10 @@
         scratch_shapes=[
             pltpu.VMEM((3, rows, width), f32), pltpu.VMEM((rows, width), jnp.int32),
             pltpu.SMEM(fold_map.shape, jnp.int32),
-            pair, pair, pair, pair, pair, pair,
-            pltpu.VMEM((8, 2, tall, width), f32),
-            pltpu.VMEM((2 * STEPS + 1, tall, width), f32),
-            pltpu.VMEM((2 * STEPS + 1, tall, width), f32),
+            pltpu.VMEM((3, tall, width), f32), pltpu.VMEM((3, tall, width), f32),
+            *tile(rows),
+            *tile(seam_rows),
+            pltpu.VMEM((2, seam_rows, width), f32),
             edge, edge, edge,
             pltpu.VMEM((2, group_rows, width), f32),
             pltpu.VMEM((2, 64, width), f32),

time: 21.8 us -> 20.5 us (0.940)
  Pallas kernels: 21 us -> 19.7 us
    pallas_call x1, Pallas kernels: 20.3 us -> 19 us  [per_device(): pl.pallas_call(functools.partial(kernel, n_lat, n_lon), out_shape=[pltpu....]
where the time goes in v2:
time: 20.5 us; the launch traced here: 20.4 us
  Pallas kernels  19.7 us (96%)
  between operations  0.64 us (3%)
    pallas_call x1, Pallas kernels, per_device(): pl.pallas_call(functools.partial(kernel, n_lat, n_lon), out_shape=[pltpu....  19 us
    pallas_call x1, Pallas kernels, per_device(): pl.pallas_call(hand_over, out_shape=[jax.ShapeDtypeStruct((rows, width),...  0.68 us

profile of v2, /device:TPU:0, one launch (start us, length us, event | category | flops | bytes accessed | tf_op | source)
XLA Modules:
  0.0 20.4 jit_solution(16112200349498272002)
XLA Ops:
  0.6 19.0 %tripole_cg.1 = (f32[160,128]{1,0:T(8,128)S(1)}, f32[160,128]{1,0:T(8,128)S(1)}) custom-call(f32[160,128]{1,0:T(8,128)} %forcing_hbm.1, f32[160,128]{1,0:T(8,128)} %search_hbm.1, f32[160,128]{1,0:T(8,128)} %depth_hbm.1, s32[160,128]{1,0:T(8,128)} %mask_hbm.1, s32[1024]{0:T(1024)} %fold_hbm.1), custom_call_target="tpu_custom_call" | custom-call | tf_op jit(solution)/shard_map/tripole_cg/pallas_call | solution.py:705
  19.7 0.7 %hand_over.1 = (f32[160,128]{1,0:T(8,128)}, f32[160,128]{1,0:T(8,128)}) custom-call(f32[160,128]{1,0:T(8,128)S(1)} %get-tuple-element.4.height, f32[160,128]{1,0:T(8,128)S(1)} %get-tuple-element.5.residual), custom_call_target="tpu_custom_call" | custom-call | tf_op jit(solution)/shard_map/hand_over/pallas_call | solution.py:730

commit v3 on v2

--- a/solution.py
+++ b/solution.py
@@ -200,7 +200,7 @@
                 add_dot(key, piece, right[8 * i : 8 * i + 8, :])
 
     row_chunks = chunks_of(8, 8 + rows, CHUNK)
-    for at, count in row_chunks:
+    for at, count in row_chunks if keep else []:
         p0 = basis[0, at : at + count, :]
         r0 = basis[STEPS + 1, at : at + count, :]
         masks = keep(at - 8, count)
@@ -235,6 +235,8 @@
                     value = value - basis[slot - 2, at : at + count, :]
                 basis[slot, at : at + count, :] = value
                 fresh[name] = value
+            if not keep:
+                continue
             masks = keep(at - 8, count)
             fresh_kept = {name: masked(masks, fresh[name]) for name, _ in chains}
             for name, _ in chains:
@@ -249,15 +251,17 @@
                     fresh_kept["p"],
                     basis[STEPS + power, at : at + count, :],
                 )
-        flush(new)
+        if keep:
+            flush(new)
 
 
 def kernel(
     n_lat, n_lon, forcing_hbm, search_hbm, depth_hbm, mask_hbm, fold_hbm,
     out_height, out_residual, loaded, mask_in, fold_map,
     centre, side, wide, wide_shifted, wide_weights, wide_basis, seam, seam_shifted,
-    seam_weights, seam_basis, patch, row_north, row_south, fold_rows, packed, got_rows, got_sides,
-    fold_all, dots, moment_rows, load_sem, near_send, near_recv, *moment_refs,
+    seam_weights, seam_basis, far, far_shifted, far_weights, far_basis, patch, row_north, row_south,
+    fold_rows, packed, got_rows, got_sides, fold_all, deep_packed, got_deep, deep_rows, got_far,
+    far_centre, far_side, dots, moment_rows, load_sem, near_send, near_recv, *moment_refs,
 ):
     rows, width = forcing_hbm.shape
     lat, lon = lax.axis_index("lat"), lax.axis_index("lon")
@@ -329,7 +333,8 @@
     packed[0] = west_edge
     packed[1] = east_edge
     first, last = PAD, PAD + rows
-    spans = ((0, 0, 16), (1, 16, 8), (2, 24, 8))
+    spans = ((0, 0, LIP), (1, LIP, STEPS), (2, LIP + STEPS, STEPS))
+    depth_of = LIP + 2 * STEPS
     for index, at, count in spans:
         row_south[at : at + count, :] = centre[index, first : first + count, :]
         row_north[at : at + count, :] = centre[index, last - count : last, :]
@@ -339,42 +344,65 @@
         for index, at, count in spans:
             for r in range(count):
                 fold_rows[at + r : at + r + 1, :] = centre[index, last - 1 - r : last - r, :]
-        fold_all[lon] = fold_rows[...]
+        fold_all[lon, 0:depth_of, :] = fold_rows[0:depth_of, :]
 
     pl.semaphore_wait(barrier, greeted)
 
-    def near(index, source, target, place):
+    half = n_lon // 2
+    at_seam, past_seam = lon == n_lon - 1, lon == 0
+    on_top = lat == top
+    fold_late, fold_early = on_top & (lon >= half), on_top & (lon < half)
+
+    def near(gone, arrived, source, target, place):
         return pltpu.make_async_remote_copy(
-            src_ref=source, dst_ref=target, send_sem=near_send.at[index],
-            recv_sem=near_recv.at[index], device_id=place, device_id_type=MESH,
+            src_ref=source, dst_ref=target, send_sem=near_send.at[gone],
+            recv_sem=near_recv.at[arrived], device_id=place, device_id_type=MESH,
         )
 
-    tail = pl.ds(group_rows - 16, 16)
-    head = pl.ds(0, 16)
-    got_south, got_north = got_rows.at[0, 0:32], got_rows.at[1, 0:32]
+    def arrival(index, block):
+        return near(0, index, block, block, (lat, lon))
+
+    def departure(index, block):
+        return near(index, 0, block, block, (lat, lon))
+
+    tail, head = pl.ds(group_rows - LIP, LIP), pl.ds(0, LIP)
+    tall_tail = pl.ds(group_rows - 2 * LIP, 2 * LIP)
+    full = pl.ds(0, depth_of)
+    near_rows = pl.ds(0, depth_of + LIP)
+    got_south, got_north = got_rows.at[0, full], got_rows.at[1, full]
     got_west, got_east = got_sides.at[0], got_sides.at[1]
-    corners = [got_rows.at[index // 2, pl.ds(32 + 16 * (index % 2), 16)] for index in range(4)]
+    corners = [got_rows.at[index // 2, pl.ds(depth_of + LIP * (index % 2), LIP)] for index in range(4)]
+    deep_strip = got_deep.at[0:group_rows]
+    deep_south = got_deep.at[group_rows : group_rows + LIP]
+    deep_north = got_deep.at[group_rows + LIP : group_rows + 2 * LIP]
+    far_rows = got_far.at[0 : 3 * LIP]
+    far_edges = [got_far.at[at : at + 2 * LIP] for at in (3 * LIP, 5 * LIP)]
     northward = (
-        near(0, row_north, got_south, (north, lon)),
-        near(0, packed.at[1, tail], corners[0], (north, east)),
-        near(0, packed.at[0, tail], corners[1], (north, west)),
+        near(0, 0, row_north.at[full], got_south, (north, lon)),
+        near(0, 0, packed.at[1, tail], corners[0], (north, east)),
+        near(0, 4, packed.at[0, tail], corners[1], (north, west)),
     )
     southward = (
-        near(1, row_south, got_north, (south, lon)),
-        near(1, packed.at[1, head], corners[2], (south, east)),
-        near(1, packed.at[0, head], corners[3], (south, west)),
+        near(1, 1, row_south.at[full], got_north, (south, lon)),
+        near(1, 1, packed.at[1, head], corners[2], (south, east)),
+        near(1, 5, packed.at[0, head], corners[3], (south, west)),
     )
-    to_east = near(2, packed.at[1], got_west, (lat, east))
-    to_west = near(2, packed.at[0], got_east, (lat, west))
-
-    def arrival(index, block):
-        return near(index, block, block, (lat, lon))
-
-    from_south, from_north = arrival(0, got_rows.at[0]), arrival(1, got_rows.at[1])
-    from_sides = arrival(2, got_sides)
-    from_fold = arrival(3, fold_all.at[0 : n_lon - 1])
-
-    def spread(source, slots, send_sem, recv_sem, along_lat):
+    to_east = near(2, 2, packed.at[1], got_west, (lat, east))
+    to_west = near(2, 3, packed.at[0], got_east, (lat, west))
+    deep_east = near(4, 7, deep_packed, deep_strip, (lat, east))
+    deep_up = near(5, 8, deep_packed.at[tail], deep_south, (north, east))
+    deep_down = near(6, 9, deep_packed.at[head], deep_north, (south, east))
+
+    def across_half(step):
+        return (lat, lax.rem(lon + step + n_lon, n_lon))
+
+    far_away = near(7, 10, deep_rows, far_rows, across_half(-half))
+    far_west_edge = near(8, 10, packed.at[1, tall_tail], far_edges[0], across_half(1 - half))
+    far_east_edge = near(9, 10, packed.at[0, tall_tail], far_edges[1], across_half(-1 - half))
+    gives_west_edge = on_top & (lon >= half - 1) & (lon < n_lon - 1)
+    gives_east_edge = on_top & ((lon > half) | (lon == 0))
+
+    def spread(source, slot, send_sem, recv_sem, along_lat):
         size = n_lat if along_lat else n_lon
         me = lat if along_lat else lon
         copies = []
@@ -382,7 +410,7 @@
             peer = lax.rem(me + d, size)
             copies.append(
                 pltpu.make_async_remote_copy(
-                    src_ref=source, dst_ref=slots.at[me], send_sem=send_sem,
+                    src_ref=source, dst_ref=slot, send_sem=send_sem,
                     recv_sem=recv_sem,
                     device_id=(peer, lon) if along_lat else (lat, peer),
                     device_id_type=MESH,
@@ -390,15 +418,12 @@
             )
         return copies
 
-    across = spread(fold_rows, fold_all, near_send.at[3], near_recv.at[3], False)
-
-    @pl.when(lat == top)
-    def _():
-        for copy in across:
-            copy.start()
-
+    across = spread(
+        fold_rows.at[full], fold_all.at[lon, full], near_send.at[3], near_recv.at[6], False
+    )
+
+    to_west.start()
     to_east.start()
-    to_west.start()
 
     @pl.when(has_north)
     def _():
@@ -408,6 +433,50 @@
     @pl.when(has_south)
     def _():
         for copy in southward:
+            copy.start()
+
+    @pl.when(at_seam)
+    def _():
+        for g in range(n_groups):
+            here = pl.ds(PAD + g * group_rows, group_rows)
+            inside = lane_group - g * GROUP
+            value = jnp.where(
+                inside < LIP,
+                turned(centre[0, here, :], g * GROUP + 2 * LIP),
+                jnp.where(
+                    inside < 2 * LIP,
+                    turned(centre[1, here, :], g * GROUP + 3 * LIP - 1),
+                    turned(centre[2, here, :], g * GROUP + 4 * LIP - 1),
+                ),
+            )
+            if g:
+                value = jnp.where(inside >= 0, value, deep_packed[...])
+            deep_packed[...] = value
+        deep_east.start()
+
+        @pl.when(has_north)
+        def _():
+            deep_up.start()
+
+        @pl.when(has_south)
+        def _():
+            deep_down.start()
+
+    @pl.when(on_top)
+    def _():
+        for index, top_row in enumerate((LIP, STEPS, STEPS)):
+            low = last - top_row - LIP
+            deep_rows[index * LIP : (index + 1) * LIP, :] = centre[index, low : low + LIP, :]
+        for copy in reversed(across):
+            copy.start()
+
+    for condition, copy in (
+        (fold_late, far_away),
+        (gives_west_edge, far_west_edge),
+        (gives_east_edge, far_east_edge),
+    ):
+        @pl.when(condition)
+        def _():
             copy.start()
 
     dot_sums = {}
@@ -435,54 +504,54 @@
 
     march(rows, wide_weights, wide_basis, keep_wide, add_dot, flush, True)
 
-    def unpack(got_e, got_w, start, g, count):
+    part_spans = ((0, 0, LIP), (1, LIP, STEPS), (2, LIP + STEPS, STEPS))
+
+    def unpack_west(got, target, start, g, count):
         lane = lax.broadcasted_iota(jnp.int32, (count, width), 1)
-        base = -g * GROUP
-        for index, offset, cells in ((0, 0, 9), (1, 9, 8), (2, 17, 8)):
-            from_east = turned(got_e, base - offset)
-            from_west = turned(got_w, base - offset - cells)
+        for index, offset, cells in part_spans:
+            value = turned(got, -g * GROUP - offset - cells)
+            target[index, start : start + count, :] = jnp.where(lane >= width - cells, value, 0.0)
+
+    def unpack_east(got, target, start, g, count):
+        lane = lax.broadcasted_iota(jnp.int32, (count, width), 1)
+        for index, offset, cells in part_spans:
+            value = turned(got, -g * GROUP - offset)
+            target[index, start : start + count, :] = jnp.where(
+                lane < cells, value, target[index, start : start + count, :]
+            )
+
+    def unpack_deep(got, start, g, count):
+        lane = lax.broadcasted_iota(jnp.int32, (count, width), 1)
+        for index, cells in ((0, LIP), (1, STEPS), (2, STEPS)):
+            low = width - cells - LIP
+            value = turned(got, low - g * GROUP - index * LIP)
             side[index, start : start + count, :] = jnp.where(
-                lane < cells,
-                from_east,
-                jnp.where(lane >= width - cells, from_west, jnp.zeros_like(got_e)),
+                (lane >= low) & (lane < low + LIP), value, side[index, start : start + count, :]
             )
 
-    for index in (1, 2):
-        for at in (0, last + 8):
+    for index in (0, 1, 2):
+        for at in (0, 8, last, last + 8):
             centre[index, at : at + 8, :] = nothing
             side[index, at : at + 8, :] = nothing
 
-    from_sides.wait_recv()
-    for g in range(n_groups):
-        unpack(got_east[...], got_west[...], PAD + g * group_rows, g, group_rows)
-
-    @pl.when(has_south)
-    def _():
-        from_south.wait_recv()
-        centre[0, 0:16, :] = got_south[0:16, :]
-        centre[1, 8:16, :] = got_south[16:24, :]
-        centre[2, 8:16, :] = got_south[24:32, :]
-        unpack(corners[1][...], corners[0][...], 0, n_groups - 1, 16)
-
-    @pl.when(lat == 0)
-    def _():
-        for target in (centre, side):
-            for index, at in ((0, 0), (0, 8), (1, 8), (2, 8)):
-                target[index, at : at + 8, :] = nothing
-
-    @pl.when(has_north)
-    def _():
-        from_north.wait_recv()
-        centre[0, last : last + 16, :] = got_north[0:16, :]
-        centre[1, last : last + 8, :] = got_north[16:24, :]
-        centre[2, last : last + 8, :] = got_north[24:32, :]
-        unpack(corners[3][...], corners[2][...], last, 0, 16)
-
-    @pl.when(lat == top)
-    def _():
-        from_fold.wait_recv()
+    def take_east():
+        arrival(3, got_east).wait_recv()
+        for g in range(n_groups):
+            unpack_east(got_east[...], side, first + g * group_rows, g, group_rows)
+
+        @pl.when(has_south)
+        def _():
+            arrival(4, corners[1]).wait_recv()
+            unpack_east(corners[1][...], side, first - LIP, n_groups - 1, LIP)
+
+        @pl.when(has_north)
+        def _():
+            arrival(5, corners[3]).wait_recv()
+            unpack_east(corners[3][...], side, last, 0, LIP)
+
+    def folded(home):
         total = n_lon * width
-        pivot = lax.rem(fold_map[0] - lon * width + total, total)
+        pivot = lax.rem(fold_map[0] - home * width + total, total)
         block, offset = pivot // width, lax.rem(pivot, width)
         lane = lax.broadcasted_iota(jnp.int32, (32, width), 1)
         index = lax.rem(offset - lane + width, width)
@@ -497,10 +566,13 @@
         halo = jnp.where(
             lane < width // 2, jnp.where(close, behind, beyond), jnp.where(close, ahead, same)
         )
-        for source, target in ((value, centre), (halo, side)):
-            target[0, last : last + 16, :] = source[0:16, :]
-            target[1, last : last + 8, :] = source[16:24, :]
-            target[2, last : last + 8, :] = source[24:32, :]
+        return value, halo
+
+    def take_fold():
+        arrival(6, fold_all.at[0 : n_lon - 1, full]).wait_recv()
+        for source, target in zip(folded(lon), (centre, side)):
+            for index, at, count in spans:
+                target[index, last : last + count, :] = source[at : at + count, :]
 
     n_parts = width // GROUP // 2
     part_rows = rows // n_parts
@@ -508,49 +580,200 @@
     seam_rows = strip_rows + 2 * BAND
     north_at, south_at = strip_rows, strip_rows + BAND
     own = GROUP - LIP
-    targets = (seam.at[0], seam_basis.at[0], seam_basis.at[STEPS + 1])
-    for index, target in enumerate(targets):
-        for at in range(0, strip_rows, 8):
-            value = None
-            for q in range(n_parts):
-                span = slice(PAD + q * part_rows - MARGIN + at, PAD + q * part_rows - MARGIN + at + 8)
-                inside, outside = centre[index, span, :], side[index, span, :]
-                east_slot = turned(
-                    jnp.where(lane8 >= width - own, inside, outside), q * GROUP - (width - own)
-                )
-                west_slot = turned(
-                    jnp.where(lane8 < own, inside, outside), (n_parts + q) * GROUP + LIP
-                )
-                if q == 0:
-                    value = jnp.where(lane8 < n_parts * GROUP, east_slot, west_slot)
-                else:
+    slot_of = lane8 // GROUP
+    slot_lane = lane8 - slot_of * GROUP
+
+    def assemble():
+        targets = (seam.at[0], seam_basis.at[0], seam_basis.at[STEPS + 1])
+        for index, target in enumerate(targets):
+            for at in range(0, strip_rows, 8):
+                value = None
+                for q in range(n_parts):
+                    low = PAD + q * part_rows - MARGIN + at
+                    inside, outside = centre[index, low : low + 8, :], side[index, low : low + 8, :]
+                    east_slot = turned(
+                        jnp.where(lane8 >= width - own, inside, outside),
+                        q * GROUP - (width - own),
+                    )
+                    west_slot = turned(
+                        jnp.where(lane8 < own, inside, outside), (n_parts + q) * GROUP + LIP
+                    )
                     mixed = jnp.where(lane8 < n_parts * GROUP, east_slot, west_slot)
-                    value = jnp.where((lane8 // GROUP) % n_parts >= q, mixed, value)
-            target[8 + at : 16 + at, :] = value
-        for at in range(0, BAND, 8):
-            low = last + LIP - BAND + at
-            target[8 + north_at + at : 16 + north_at + at, :] = centre[index, low : low + 8, :]
-            low = first - LIP + at
-            target[8 + south_at + at : 16 + south_at + at, :] = centre[index, low : low + 8, :]
-
-    prepare(seam_rows, seam, seam_shifted, seam_weights, seam_basis)
-    slot_lane = lax.rem(lane8, GROUP)
+                    value = mixed if q == 0 else jnp.where(
+                        lax.rem(slot_of, n_parts) >= q, mixed, value
+                    )
+                target[8 + at : 16 + at, :] = value
+            for at in range(0, BAND, 8):
+                low = last + LIP - BAND + at
+                target[8 + north_at + at : 16 + north_at + at, :] = centre[index, low : low + 8, :]
+                low = first - LIP + at
+                target[8 + south_at + at : 16 + south_at + at, :] = centre[index, low : low + 8, :]
+        prepare(seam_rows, seam, seam_shifted, seam_weights, seam_basis)
+
+    arrival(2, got_west).wait_recv()
+    for g in range(n_groups):
+        unpack_west(got_west[...], side, first + g * group_rows, g, group_rows)
+
+    @pl.when(has_south)
+    def _():
+        arrival(0, got_rows.at[0, near_rows]).wait_recv()
+        for index, at, count in spans:
+            centre[index, first - count : first, :] = got_south[at : at + count, :]
+        unpack_west(corners[0][...], side, first - LIP, n_groups - 1, LIP)
+
+    @pl.when(has_north)
+    def _():
+        arrival(1, got_rows.at[1, near_rows]).wait_recv()
+        for index, at, count in spans:
+            centre[index, last : last + count, :] = got_north[at : at + count, :]
+        unpack_west(corners[2][...], side, last, 0, LIP)
+
+    @pl.when(jnp.logical_not(at_seam))
+    def _():
+        take_east()
+
+    @pl.when(fold_early)
+    def _():
+        take_fold()
+
+    assemble()
     east_half = lane8 < n_parts * GROUP
-    strip_lanes = jnp.where(east_half, slot_lane - (own - LIP), slot_lane - LIP)
-    strip_lanes = (strip_lanes >= 0) & (strip_lanes < LIP)
+    strip_at = jnp.where(east_half, slot_lane - (own - LIP), slot_lane - LIP)
+    closed = jnp.where(fold_late, 1, 0)
+    strip_lanes = (strip_at >= 0) & (strip_at < LIP) & (
+        jnp.where(east_half, lon, -1) < n_lon - 1
+    )
+    last_part = lax.rem(slot_of, n_parts) == n_parts - 1
+    north_lanes = strip_lanes & (jnp.where(last_part, closed, 0) == 0)
+    band_lanes = jnp.where(middle, closed, 1) == 0
 
     def keep_seam(at, count):
         return kept(
             at,
             count,
             [
-                (MARGIN, MARGIN + part_rows, strip_lanes),
-                (north_at + BAND - 2 * LIP, north_at + BAND - LIP, middle),
+                (MARGIN, MARGIN + part_rows - LIP, strip_lanes),
+                (MARGIN + part_rows - LIP, MARGIN + part_rows, north_lanes),
+                (north_at + BAND - 2 * LIP, north_at + BAND - LIP, band_lanes),
                 (south_at + LIP, south_at + 2 * LIP, middle),
             ],
         )
 
     march(seam_rows, seam_weights, seam_basis, keep_seam, add_dot, flush, False)
+
+    patch_rows = group_rows + 2 * MARGIN
+    far_tile_rows = patch_rows + 2 * BAND
+
+    @pl.when(past_seam | fold_early)
+    def _():
+        @pl.when(past_seam)
+        def _():
+            arrival(7, deep_strip).wait_recv()
+            for g in range(n_groups):
+                unpack_deep(deep_strip[...], first + g * group_rows, g, group_rows)
+
+            @pl.when(has_south)
+            def _():
+                arrival(8, deep_south).wait_recv()
+                unpack_deep(deep_south[...], first - LIP, n_groups - 1, LIP)
+
+            @pl.when(has_north)
+            def _():
+                arrival(9, deep_north).wait_recv()
+                unpack_deep(deep_north[...], last, 0, LIP)
+
+        for target in (far_centre, far_side):
+            for index in (0, 1, 2):
+                for at in range(0, BAND, 8):
+                    target[index, at : at + 8, :] = nothing
+
+        edge_row = BAND - LIP
+
+        @pl.when(fold_early)
+        def _():
+            arrival(10, got_far).wait_recv()
+            home = lon + half
+            low = edge_row - 2 * LIP
+            unpack_west(far_edges[0][...], far_side, low, n_groups - 1, 2 * LIP)
+            unpack_east(far_edges[1][...], far_side, low, n_groups - 1, 2 * LIP)
+            mirror = folded(home)
+            for index, at, count in spans:
+                low = edge_row - count - LIP
+                far_centre[index, low : low + LIP, :] = far_rows[
+                    index * LIP : (index + 1) * LIP, :
+                ]
+                for r in range(count):
+                    far_centre[index, edge_row - 1 - r : edge_row - r, :] = fold_all[
+                        home, at + r : at + r + 1, :
+                    ]
+                for source, target in zip(mirror, (far_centre, far_side)):
+                    target[index, edge_row : edge_row + count, :] = source[at : at + count, :]
+
+        span_lanes = GROUP - 2 * LIP
+        targets = (far.at[0], far_basis.at[0], far_basis.at[STEPS + 1])
+        for index, target in enumerate(targets):
+            for at in range(0, patch_rows, 8):
+                value = None
+                for g in range(n_groups):
+                    low = PAD + g * group_rows - MARGIN + at
+                    mixed = turned(
+                        jnp.where(
+                            lane8 < span_lanes,
+                            centre[index, low : low + 8, :],
+                            side[index, low : low + 8, :],
+                        ),
+                        g * GROUP + 2 * LIP,
+                    )
+                    value = mixed if g == 0 else jnp.where(slot_of >= g, mixed, value)
+                target[8 + at : 16 + at, :] = value
+            for at in range(0, BAND, 8):
+                inside, outside = far_centre[index, at : at + 8, :], far_side[index, at : at + 8, :]
+                spot = 8 + patch_rows + at
+                target[spot : spot + 8, :] = inside
+                spot += BAND
+                target[spot : spot + 8, :] = jnp.where(
+                    lane8 < GROUP,
+                    turned(jnp.where(lane8 >= width - own, inside, outside), own - width),
+                    turned(jnp.where(lane8 < own, inside, outside), GROUP + LIP),
+                )
+        prepare(far_tile_rows, far, far_shifted, far_weights, far_basis)
+        patch_lanes = jnp.where((slot_lane >= LIP) & (slot_lane < 2 * LIP), lon, 1) == 0
+        upper = jnp.where(slot_of == n_groups - 1, jnp.where(on_top, 1, 0), 0) == 0
+        idle = jnp.where(fold_early, 0, 1)
+        fold_lanes = jnp.where(middle, idle, 1) == 0
+        edge_at = jnp.where(slot_of == 0, slot_lane - (own - LIP), slot_lane - LIP)
+        edge_lanes = jnp.where(
+            (slot_of < 2) & (edge_at >= 0) & (edge_at < LIP), idle, 1
+        ) == 0
+
+        def keep_far(at, count):
+            fold_at = patch_rows + BAND - 2 * LIP
+            return kept(
+                at,
+                count,
+                [
+                    (MARGIN, MARGIN + group_rows - LIP, patch_lanes),
+                    (MARGIN + group_rows - LIP, MARGIN + group_rows, patch_lanes & upper),
+                    (fold_at, fold_at + LIP, fold_lanes),
+                    (fold_at + BAND, fold_at + BAND + LIP, edge_lanes),
+                ],
+            )
+
+        march(far_tile_rows, far_weights, far_basis, keep_far, add_dot, flush, False)
+
+    def finish_late():
+        @pl.when(at_seam | fold_late)
+        def _():
+            @pl.when(at_seam)
+            def _():
+                take_east()
+
+            @pl.when(fold_late)
+            def _():
+                take_fold()
+
+            assemble()
+            march(seam_rows, seam_weights, seam_basis, None, None, None, False)
 
     number = len(order_of())
     pending = []
@@ -585,9 +808,11 @@
         if copies is None:
             me, along_lat = rest
             slots[me] = message
-            copies = spread(slots.at[me], slots, send_sem, recv_sem, along_lat)
+            copies = spread(slots.at[me], slots.at[me], send_sem, recv_sem, along_lat)
         for copy in copies:
             copy.start()
+        if not pending:
+            finish_late()
         others = slots.at[0 : size - 1]
         whole = pltpu.make_async_remote_copy(
             src_ref=others, dst_ref=others, send_sem=send_sem, recv_sem=recv_sem,
@@ -653,19 +878,21 @@
 
     for copy in pending:
         copy.wait_send()
-    from_sides.wait_send()
-
-    @pl.when(has_north)
-    def _():
-        from_south.wait_send()
-
-    @pl.when(has_south)
-    def _():
-        from_north.wait_send()
-
-    @pl.when(lat == top)
-    def _():
-        from_fold.wait_send()
+    departure(2, got_sides).wait_send()
+    for condition, index, block in (
+        (has_north, 0, got_rows.at[0]),
+        (has_south, 1, got_rows.at[1]),
+        (on_top, 3, fold_all.at[0 : n_lon - 1, full]),
+        (at_seam, 4, deep_packed),
+        (at_seam & has_north, 5, deep_south),
+        (at_seam & has_south, 6, deep_north),
+        (fold_late, 7, far_rows),
+        (gives_west_edge, 8, far_edges[0]),
+        (gives_east_edge, 9, far_edges[1]),
+    ):
+        @pl.when(condition)
+        def _():
+            departure(index, block).wait_send()
 
 
 @functools.cache
@@ -713,15 +940,21 @@
             pltpu.VMEM((3, tall, width), f32), pltpu.VMEM((3, tall, width), f32),
             *tile(rows),
             *tile(seam_rows),
+            *tile(group_rows + 2 * MARGIN + 2 * BAND),
             pltpu.VMEM((2, seam_rows, width), f32),
             edge, edge, edge,
             pltpu.VMEM((2, group_rows, width), f32),
-            pltpu.VMEM((2, 64, width), f32),
+            pltpu.VMEM((2, 3 * LIP + 2 * STEPS, width), f32),
             pltpu.VMEM((2, group_rows, width), f32),
             pltpu.VMEM((n_lon, 32, width), f32),
+            pltpu.VMEM((group_rows, width), f32),
+            pltpu.VMEM((group_rows + 2 * LIP, width), f32),
+            pltpu.VMEM((3 * LIP, width), f32),
+            pltpu.VMEM((7 * LIP, width), f32),
+            pltpu.VMEM((3, BAND, width), f32), pltpu.VMEM((3, BAND, width), f32),
             pltpu.VMEM((6 * STEPS, 8, width), f32),
             pltpu.VMEM((6 * STEPS, width), f32),
-            dma((3,)), dma((4,)), dma((4,)),
+            dma((3,)), dma((10,)), dma((11,)),
             *moment_refs,
         ],
         compiler_params=pltpu.CompilerParams(collective_id=0, has_side_effects=True),

time: 20.5 us -> 19.4 us (0.946)
  Pallas kernels: 19.7 us -> 18.6 us
    pallas_call x1, Pallas kernels: 19 us -> 17.9 us  [per_device(): pl.pallas_call(functools.partial(kernel, n_lat, n_lon), out_shape=[pltpu....]
where the time goes in v3:
time: 19.4 us; the launch traced here: 19.2 us
  Pallas kernels  18.6 us (96%)
  between operations  0.64 us (3%)
    pallas_call x1, Pallas kernels, per_device(): pl.pallas_call(functools.partial(kernel, n_lat, n_lon), out_shape=[pltpu....  17.9 us
    pallas_call x1, Pallas kernels, per_device(): pl.pallas_call(hand_over, out_shape=[jax.ShapeDtypeStruct((rows, width),...  0.68 us

profile of v3, /device:TPU:0, one launch (start us, length us, event | category | flops | bytes accessed | tf_op | source)
XLA Modules:
  0.0 19.2 jit_solution(9461522528948724404)
XLA Ops:
  0.6 17.9 %tripole_cg.1 = (f32[160,128]{1,0:T(8,128)S(1)}, f32[160,128]{1,0:T(8,128)S(1)}) custom-call(f32[160,128]{1,0:T(8,128)} %forcing_hbm.1, f32[160,128]{1,0:T(8,128)} %search_hbm.1, f32[160,128]{1,0:T(8,128)} %depth_hbm.1, s32[160,128]{1,0:T(8,128)} %mask_hbm.1, s32[1024]{0:T(1024)} %fold_hbm.1), custom_call_target="tpu_custom_call" | custom-call | tf_op jit(solution)/shard_map/tripole_cg/pallas_call | solution.py:932
  18.5 0.7 %hand_over.1 = (f32[160,128]{1,0:T(8,128)}, f32[160,128]{1,0:T(8,128)}) custom-call(f32[160,128]{1,0:T(8,128)S(1)} %get-tuple-element.4.height, f32[160,128]{1,0:T(8,128)S(1)} %get-tuple-element.5.residual), custom_call_target="tpu_custom_call" | custom-call | tf_op jit(solution)/shard_map/hand_over/pallas_call | solution.py:963

commit v4 on v3

--- a/solution.py
+++ b/solution.py
@@ -187,7 +187,25 @@
                 ) * (link * from_root)
 
 
-def march(rows, weights, basis, keep, add_dot, flush, new):
+def needed(rows, regions, reach):
+    tiles = sorted({
+        at
+        for low, high, _ in regions
+        for at in range(max(low - reach, 0) // 8 * 8, min(high + reach, rows), 8)
+    })
+    runs = []
+    for at in tiles:
+        if runs and runs[-1][0] + runs[-1][1] == at and runs[-1][1] < CHUNK:
+            runs[-1][1] += 8
+        else:
+            runs.append([at, 8])
+    return [(8 + at, count) for at, count in runs]
+
+
+def march(rows, weights, basis, regions, add_dot, flush, new):
+    def keep(at, count):
+        return kept(at, count, regions)
+
     def masked(masks, value):
         return [
             None if mask is None else jnp.where(mask, value[8 * i : 8 * i + 8, :], 0.0)
@@ -199,8 +217,7 @@
             if piece is not None:
                 add_dot(key, piece, right[8 * i : 8 * i + 8, :])
 
-    row_chunks = chunks_of(8, 8 + rows, CHUNK)
-    for at, count in row_chunks if keep else []:
+    for at, count in needed(rows, regions, 0) if add_dot else []:
         p0 = basis[0, at : at + count, :]
         r0 = basis[STEPS + 1, at : at + count, :]
         masks = keep(at - 8, count)
@@ -211,7 +228,7 @@
 
     for power in range(1, STEPS + 1):
         chains = [("p", 0)] + ([("r", STEPS + 1)] if power < STEPS else [])
-        for at, count in row_chunks:
+        for at, count in needed(rows, regions, STEPS - power):
             fresh = {}
             held = {}
             factors = {ab: weights[SLOT[ab], at : at + count, :] for ab in DIRECTIONS}
@@ -235,7 +252,7 @@
                     value = value - basis[slot - 2, at : at + count, :]
                 basis[slot, at : at + count, :] = value
                 fresh[name] = value
-            if not keep:
+            if not add_dot:
                 continue
             masks = keep(at - 8, count)
             fresh_kept = {name: masked(masks, fresh[name]) for name, _ in chains}
@@ -251,7 +268,7 @@
                     fresh_kept["p"],
                     basis[STEPS + power, at : at + count, :],
                 )
-        if keep:
+        if add_dot:
             flush(new)
 
 
@@ -351,7 +368,7 @@
     half = n_lon // 2
     at_seam, past_seam = lon == n_lon - 1, lon == 0
     on_top = lat == top
-    fold_late, fold_early = on_top & (lon >= half), on_top & (lon < half)
+    fold_late, fold_early = on_top & (lon > half), on_top & (lon >= 1) & (lon < half)
 
     def near(gone, arrived, source, target, place):
         return pltpu.make_async_remote_copy(
@@ -399,8 +416,8 @@
     far_away = near(7, 10, deep_rows, far_rows, across_half(-half))
     far_west_edge = near(8, 10, packed.at[1, tall_tail], far_edges[0], across_half(1 - half))
     far_east_edge = near(9, 10, packed.at[0, tall_tail], far_edges[1], across_half(-1 - half))
-    gives_west_edge = on_top & (lon >= half - 1) & (lon < n_lon - 1)
-    gives_east_edge = on_top & ((lon > half) | (lon == 0))
+    gives_west_edge = on_top & (lon >= half) & (lon < n_lon - 1)
+    gives_east_edge = on_top & ((lon > half + 1) | (lon == 0))
 
     def spread(source, slot, send_sem, recv_sem, along_lat):
         size = n_lat if along_lat else n_lon
@@ -499,10 +516,9 @@
     prepare(rows, wide, wide_shifted, wide_weights, wide_basis)
     middle = (lane8 >= LIP) & (lane8 < width - LIP)
 
-    def keep_wide(at, count):
-        return kept(at, count, [(LIP, rows - LIP, middle)])
-
-    march(rows, wide_weights, wide_basis, keep_wide, add_dot, flush, True)
+    march(
+        rows, wide_weights, wide_basis, [(LIP, rows - LIP, middle)], add_dot, flush, True
+    )
 
     part_spans = ((0, 0, LIP), (1, LIP, STEPS), (2, LIP + STEPS, STEPS))
 
@@ -632,7 +648,7 @@
     def _():
         take_east()
 
-    @pl.when(fold_early)
+    @pl.when(on_top & (lon <= half))
     def _():
         take_fold()
 
@@ -647,71 +663,40 @@
     north_lanes = strip_lanes & (jnp.where(last_part, closed, 0) == 0)
     band_lanes = jnp.where(middle, closed, 1) == 0
 
-    def keep_seam(at, count):
-        return kept(
-            at,
-            count,
-            [
-                (MARGIN, MARGIN + part_rows - LIP, strip_lanes),
-                (MARGIN + part_rows - LIP, MARGIN + part_rows, north_lanes),
-                (north_at + BAND - 2 * LIP, north_at + BAND - LIP, band_lanes),
-                (south_at + LIP, south_at + 2 * LIP, middle),
-            ],
-        )
-
-    march(seam_rows, seam_weights, seam_basis, keep_seam, add_dot, flush, False)
+    seam_regions = [
+        (MARGIN, MARGIN + part_rows - LIP, strip_lanes),
+        (MARGIN + part_rows - LIP, MARGIN + part_rows, north_lanes),
+        (north_at + BAND - 2 * LIP, north_at + BAND - LIP, band_lanes),
+        (south_at + LIP, south_at + 2 * LIP, middle),
+    ]
+    march(seam_rows, seam_weights, seam_basis, seam_regions, add_dot, flush, False)
 
     patch_rows = group_rows + 2 * MARGIN
-    far_tile_rows = patch_rows + 2 * BAND
-
-    @pl.when(past_seam | fold_early)
-    def _():
-        @pl.when(past_seam)
+    far_tile_rows = max(patch_rows, 2 * BAND)
+    far_targets = (far.at[0], far_basis.at[0], far_basis.at[STEPS + 1])
+
+    def march_far(regions):
+        prepare(far_tile_rows, far, far_shifted, far_weights, far_basis)
+        march(far_tile_rows, far_weights, far_basis, regions, add_dot, flush, False)
+
+    @pl.when(past_seam)
+    def _():
+        arrival(7, deep_strip).wait_recv()
+        for g in range(n_groups):
+            unpack_deep(deep_strip[...], first + g * group_rows, g, group_rows)
+
+        @pl.when(has_south)
         def _():
-            arrival(7, deep_strip).wait_recv()
-            for g in range(n_groups):
-                unpack_deep(deep_strip[...], first + g * group_rows, g, group_rows)
-
-            @pl.when(has_south)
-            def _():
-                arrival(8, deep_south).wait_recv()
-                unpack_deep(deep_south[...], first - LIP, n_groups - 1, LIP)
-
-            @pl.when(has_north)
-            def _():
-                arrival(9, deep_north).wait_recv()
-                unpack_deep(deep_north[...], last, 0, LIP)
-
-        for target in (far_centre, far_side):
-            for index in (0, 1, 2):
-                for at in range(0, BAND, 8):
-                    target[index, at : at + 8, :] = nothing
-
-        edge_row = BAND - LIP
-
-        @pl.when(fold_early)
+            arrival(8, deep_south).wait_recv()
+            unpack_deep(deep_south[...], first - LIP, n_groups - 1, LIP)
+
+        @pl.when(has_north)
         def _():
-            arrival(10, got_far).wait_recv()
-            home = lon + half
-            low = edge_row - 2 * LIP
-            unpack_west(far_edges[0][...], far_side, low, n_groups - 1, 2 * LIP)
-            unpack_east(far_edges[1][...], far_side, low, n_groups - 1, 2 * LIP)
-            mirror = folded(home)
-            for index, at, count in spans:
-                low = edge_row - count - LIP
-                far_centre[index, low : low + LIP, :] = far_rows[
-                    index * LIP : (index + 1) * LIP, :
-                ]
-                for r in range(count):
-                    far_centre[index, edge_row - 1 - r : edge_row - r, :] = fold_all[
-                        home, at + r : at + r + 1, :
-                    ]
-                for source, target in zip(mirror, (far_centre, far_side)):
-                    target[index, edge_row : edge_row + count, :] = source[at : at + count, :]
+            arrival(9, deep_north).wait_recv()
+            unpack_deep(deep_north[...], last, 0, LIP)
 
         span_lanes = GROUP - 2 * LIP
-        targets = (far.at[0], far_basis.at[0], far_basis.at[STEPS + 1])
-        for index, target in enumerate(targets):
+        for index, target in enumerate(far_targets):
             for at in range(0, patch_rows, 8):
                 value = None
                 for g in range(n_groups):
@@ -726,40 +711,52 @@
                     )
                     value = mixed if g == 0 else jnp.where(slot_of >= g, mixed, value)
                 target[8 + at : 16 + at, :] = value
+        patch_lanes = (slot_lane >= LIP) & (slot_lane < 2 * LIP)
+        upper = jnp.where(slot_of == n_groups - 1, jnp.where(on_top, 1, 0), 0) == 0
+        march_far([
+            (MARGIN, MARGIN + group_rows - LIP, patch_lanes),
+            (MARGIN + group_rows - LIP, MARGIN + group_rows, patch_lanes & upper),
+        ])
+
+    @pl.when(fold_early)
+    def _():
+        edge_row = BAND - LIP
+        for target in (far_centre, far_side):
+            for index in (0, 1, 2):
+                for at in range(0, BAND, 8):
+                    target[index, at : at + 8, :] = nothing
+        arrival(10, got_far).wait_recv()
+        home = lon + half
+        low = edge_row - 2 * LIP
+        unpack_west(far_edges[0][...], far_side, low, n_groups - 1, 2 * LIP)
+        unpack_east(far_edges[1][...], far_side, low, n_groups - 1, 2 * LIP)
+        mirror = folded(home)
+        for index, at, count in spans:
+            low = edge_row - count - LIP
+            far_centre[index, low : low + LIP, :] = far_rows[index * LIP : (index + 1) * LIP, :]
+            for r in range(count):
+                far_centre[index, edge_row - 1 - r : edge_row - r, :] = fold_all[
+                    home, at + r : at + r + 1, :
+                ]
+            for source, target in zip(mirror, (far_centre, far_side)):
+                target[index, edge_row : edge_row + count, :] = source[at : at + count, :]
+        for index, target in enumerate(far_targets):
             for at in range(0, BAND, 8):
                 inside, outside = far_centre[index, at : at + 8, :], far_side[index, at : at + 8, :]
-                spot = 8 + patch_rows + at
-                target[spot : spot + 8, :] = inside
-                spot += BAND
+                target[8 + at : 16 + at, :] = inside
+                spot = 8 + BAND + at
                 target[spot : spot + 8, :] = jnp.where(
                     lane8 < GROUP,
                     turned(jnp.where(lane8 >= width - own, inside, outside), own - width),
                     turned(jnp.where(lane8 < own, inside, outside), GROUP + LIP),
                 )
-        prepare(far_tile_rows, far, far_shifted, far_weights, far_basis)
-        patch_lanes = jnp.where((slot_lane >= LIP) & (slot_lane < 2 * LIP), lon, 1) == 0
-        upper = jnp.where(slot_of == n_groups - 1, jnp.where(on_top, 1, 0), 0) == 0
-        idle = jnp.where(fold_early, 0, 1)
-        fold_lanes = jnp.where(middle, idle, 1) == 0
         edge_at = jnp.where(slot_of == 0, slot_lane - (own - LIP), slot_lane - LIP)
-        edge_lanes = jnp.where(
-            (slot_of < 2) & (edge_at >= 0) & (edge_at < LIP), idle, 1
-        ) == 0
-
-        def keep_far(at, count):
-            fold_at = patch_rows + BAND - 2 * LIP
-            return kept(
-                at,
-                count,
-                [
-                    (MARGIN, MARGIN + group_rows - LIP, patch_lanes),
-                    (MARGIN + group_rows - LIP, MARGIN + group_rows, patch_lanes & upper),
-                    (fold_at, fold_at + LIP, fold_lanes),
-                    (fold_at + BAND, fold_at + BAND + LIP, edge_lanes),
-                ],
-            )
-
-        march(far_tile_rows, far_weights, far_basis, keep_far, add_dot, flush, False)
+        edge_lanes = (slot_of < 2) & (edge_at >= 0) & (edge_at < LIP)
+        fold_at = BAND - 2 * LIP
+        march_far([
+            (fold_at, fold_at + LIP, middle),
+            (fold_at + BAND, fold_at + BAND + LIP, edge_lanes),
+        ])
 
     def finish_late():
         @pl.when(at_seam | fold_late)
@@ -773,7 +770,7 @@
                 take_fold()
 
             assemble()
-            march(seam_rows, seam_weights, seam_basis, None, None, None, False)
+            march(seam_rows, seam_weights, seam_basis, seam_regions, None, None, False)
 
     number = len(order_of())
     pending = []
@@ -940,7 +937,7 @@
             pltpu.VMEM((3, tall, width), f32), pltpu.VMEM((3, tall, width), f32),
             *tile(rows),
             *tile(seam_rows),
-            *tile(group_rows + 2 * MARGIN + 2 * BAND),
+            *tile(max(group_rows + 2 * MARGIN, 2 * BAND)),
             pltpu.VMEM((2, seam_rows, width), f32),
             edge, edge, edge,
             pltpu.VMEM((2, group_rows, width), f32),

time: 19.4 us -> 18.8 us (0.969)
  Pallas kernels: 18.6 us -> 18 us
    pallas_call x1, Pallas kernels: 17.9 us -> 17.3 us  [per_device(): pl.pallas_call(functools.partial(kernel, n_lat, n_lon), out_shape=[pltpu....]
where the time goes in v4:
time: 18.8 us; the launch traced here: 18.7 us
  Pallas kernels  18 us (96%)
  between operations  0.64 us (3%)
    pallas_call x1, Pallas kernels, per_device(): pl.pallas_call(functools.partial(kernel, n_lat, n_lon), out_shape=[pltpu....  17.3 us
    pallas_call x1, Pallas kernels, per_device(): pl.pallas_call(hand_over, out_shape=[jax.ShapeDtypeStruct((rows, width),...  0.68 us

profile of v4, /device:TPU:0, one launch (start us, length us, event | category | flops | bytes accessed | tf_op | source)
XLA Modules:
  0.0 18.7 jit_solution(7791382824829671690)
XLA Ops:
  0.6 17.3 %tripole_cg.1 = (f32[160,128]{1,0:T(8,128)S(1)}, f32[160,128]{1,0:T(8,128)S(1)}) custom-call(f32[160,128]{1,0:T(8,128)} %forcing_hbm.1, f32[160,128]{1,0:T(8,128)} %search_hbm.1, f32[160,128]{1,0:T(8,128)} %depth_hbm.1, s32[160,128]{1,0:T(8,128)} %mask_hbm.1, s32[1024]{0:T(1024)} %fold_hbm.1), custom_call_target="tpu_custom_call" | custom-call | tf_op jit(solution)/shard_map/tripole_cg/pallas_call | solution.py:929
  18.0 0.7 %hand_over.1 = (f32[160,128]{1,0:T(8,128)}, f32[160,128]{1,0:T(8,128)}) custom-call(f32[160,128]{1,0:T(8,128)S(1)} %get-tuple-element.4.height, f32[160,128]{1,0:T(8,128)S(1)} %get-tuple-element.5.residual), custom_call_target="tpu_custom_call" | custom-call | tf_op jit(solution)/shard_map/hand_over/pallas_call | solution.py:960

commit v5 on v4

--- a/solution.py
+++ b/solution.py
@@ -15,6 +15,7 @@
 CHUNK = 16
 LIP = STEPS + 1
 MARGIN = 12
+SLAB = 40
 BAND = 32
 DIRECT_LIMIT = 64
 
@@ -33,18 +34,6 @@
 def turned(x, shift):
     shift = shift % x.shape[1]
     return x if shift == 0 else pltpu.roll(x, shift, 1)
-
-
-def bilinear(left, right, gram):
-    total = None
-    for i in sorted(left):
-        inner = None
-        for j in sorted(right):
-            term = gram(i, j) * right[j]
-            inner = term if inner is None else inner + term
-        inner = left[i] * inner
-        total = inner if total is None else total + inner
-    return total
 
 
 def plus(left, right):
@@ -73,33 +62,54 @@
     return result
 
 
+def tree_sum(terms):
+    terms = list(terms)
+    while len(terms) > 1:
+        odd = terms[len(terms) // 2 * 2 :]
+        terms = [x + y for x, y in zip(terms[0::2], terms[1::2])] + odd
+    return terms[0]
+
+
+def against(coords, series):
+    return tree_sum(value * series[key] for key, value in sorted(coords.items()))
+
+
+def shifted_series(series, chain, reach):
+    result = {}
+    for k in range(reach + 1):
+        beside = (
+            series[(chain, 1)]
+            if k == 0
+            else 0.5 * (series[(chain, k + 1)] + series[(chain, k - 1)])
+        )
+        result[(chain, k)] = series[(chain, k)] + beside
+    return result
+
+
 def coordinates(moments):
-    cache = {}
-
-    def gram(left, right):
-        kind = (left[0], right[0]) if left[0] <= right[0] else (right[0], left[0])
-        low, high = sorted((left[1], right[1]))
-        key = (kind, low, high)
-        if key not in cache:
-            series = moments[kind]
-            cache[key] = 0.5 * (series[high + low] + series[high - low])
-        return cache[key]
-
+    one = jnp.ones_like(moments[("p", "p")][0])
+    direction_coords, residual_coords = {("p", 0): one}, {("r", 0): one}
+    direction = {("p", k): value for k, value in enumerate(moments[("p", "p")])}
+    direction |= {("r", k): value for k, value in enumerate(moments[("p", "r")])}
+    residual = {("p", k): value for k, value in enumerate(moments[("p", "r")])}
+    residual |= {("r", k): value for k, value in enumerate(moments[("r", "r")])}
     solution_coords = {}
-    one = jnp.ones_like(moments[("p", "p")][0])
-    direction_coords = {("p", 0): one}
-    residual_coords = {("r", 0): one}
-    norm_now = bilinear(residual_coords, residual_coords, gram)
-    for _ in range(STEPS):
-        mapped = apply_shift(direction_coords)
-        step_length = norm_now / bilinear(direction_coords, mapped, gram)
+    norm_now = residual[("r", 0)]
+    for step in range(STEPS):
+        reach = 2 * STEPS - 2 - step
+        mapped = shifted_series(direction, "p", reach) | shifted_series(direction, "r", reach - 1)
+        mapped_coords = apply_shift(direction_coords)
+        step_length = norm_now / against(direction_coords, mapped)
         solution_coords = plus(solution_coords, scaled(step_length, direction_coords))
-        residual_coords = plus(residual_coords, scaled(-step_length, mapped))
-        norm_next = bilinear(residual_coords, residual_coords, gram)
-        direction_coords = plus(
-            residual_coords, scaled(norm_next / norm_now, direction_coords)
-        )
-        norm_now = norm_next
+        residual_coords = plus(residual_coords, scaled(-step_length, mapped_coords))
+        if step == STEPS - 1:
+            break
+        residual = {key: residual[key] - step_length * value for key, value in mapped.items()}
+        shrink = 1.0 / norm_now
+        norm_now = against(residual_coords, residual)
+        turn = norm_now * shrink
+        direction = {key: value + turn * direction[key] for key, value in residual.items()}
+        direction_coords = plus(residual_coords, scaled(turn, direction_coords))
     return solution_coords, residual_coords
 
 
@@ -274,11 +284,11 @@
 
 def kernel(
     n_lat, n_lon, forcing_hbm, search_hbm, depth_hbm, mask_hbm, fold_hbm,
-    out_height, out_residual, loaded, mask_in, fold_map,
-    centre, side, wide, wide_shifted, wide_weights, wide_basis, seam, seam_shifted,
-    seam_weights, seam_basis, far, far_shifted, far_weights, far_basis, patch, row_north, row_south,
+    wide_basis, seam_basis, sums_out, loaded, mask_in, fold_map,
+    centre, side, wide, wide_shifted, wide_weights, seam, seam_shifted,
+    seam_weights, far, far_shifted, far_weights, far_basis, row_north, row_south,
     fold_rows, packed, got_rows, got_sides, fold_all, deep_packed, got_deep, deep_rows, got_far,
-    far_centre, far_side, dots, moment_rows, load_sem, near_send, near_recv, *moment_refs,
+    far_centre, far_side, dots, load_sem, near_send, near_recv, *moment_refs,
 ):
     rows, width = forcing_hbm.shape
     lat, lon = lax.axis_index("lat"), lax.axis_index("lon")
@@ -822,7 +832,48 @@
             terms = [x + y for x, y in zip(terms[0::2], terms[1::2])] + odd
         message = terms[0]
         pending.append(whole)
-    message = jnp.broadcast_to(message, (8, width))
+    sums_out[...] = jnp.broadcast_to(message, (8, width))
+    for copy in pending:
+        copy.wait_send()
+    departure(2, got_sides).wait_send()
+    for condition, index, block in (
+        (has_north, 0, got_rows.at[0]),
+        (has_south, 1, got_rows.at[1]),
+        (on_top, 3, fold_all.at[0 : n_lon - 1, full]),
+        (at_seam, 4, deep_packed),
+        (at_seam & has_north, 5, deep_south),
+        (at_seam & has_south, 6, deep_north),
+        (fold_late, 7, far_rows),
+        (gives_west_edge, 8, far_edges[0]),
+        (gives_east_edge, 9, far_edges[1]),
+    ):
+        @pl.when(condition)
+        def _():
+            departure(index, block).wait_send()
+
+
+@functools.cache
+def order_of():
+    keys = [("p", "p", k) for k in range(2 * STEPS + 1)]
+    keys += [("p", "r", k) for k in range(2 * STEPS)]
+    keys += [("r", "r", k) for k in range(2 * STEPS - 1)]
+    return {key: index for index, key in enumerate(keys)}
+
+
+def finish(
+    sums, wide_basis, seam_basis, out_height, out_residual, moment_rows, patch, results, out_sem
+):
+    rows, width = out_height.shape
+    number = len(order_of())
+    n_parts = width // GROUP // 2
+    part_rows = rows // n_parts
+    north_at = part_rows + 2 * MARGIN
+    south_at = north_at + BAND
+    seam_rows = south_at + BAND
+    own = GROUP - LIP
+    lane8 = lax.broadcasted_iota(jnp.int32, (8, width), 1)
+    home = lane8 - lax.broadcasted_iota(jnp.int32, (8, width), 0)
+    message = sums[...]
     for g in range(number // 8):
         picked = jnp.sum(jnp.where(home == 8 * g, message, 0.0), axis=1, keepdims=True)
         moment_rows[8 * g : 8 * g + 8, :] = jnp.broadcast_to(picked, (8, width))
@@ -835,6 +886,7 @@
             series.append(value if index < 2 else 2.0 * value - series[index % 2])
         moments[kind] = series
     height_coords, residual_coords = coordinates(moments)
+    outs = (out_height, out_residual)
     wanted = (height_coords, residual_coords)
 
     def combined(fields, at):
@@ -871,38 +923,16 @@
             total = jnp.where(
                 lane8 >= width - LIP, turned(strip, width - own - q * GROUP), total
             )
-            (out_height, out_residual)[which][at : at + 8, :] = total
-
-    for copy in pending:
-        copy.wait_send()
-    departure(2, got_sides).wait_send()
-    for condition, index, block in (
-        (has_north, 0, got_rows.at[0]),
-        (has_south, 1, got_rows.at[1]),
-        (on_top, 3, fold_all.at[0 : n_lon - 1, full]),
-        (at_seam, 4, deep_packed),
-        (at_seam & has_north, 5, deep_south),
-        (at_seam & has_south, 6, deep_north),
-        (fold_late, 7, far_rows),
-        (gives_west_edge, 8, far_edges[0]),
-        (gives_east_edge, 9, far_edges[1]),
-    ):
-        @pl.when(condition)
-        def _():
-            departure(index, block).wait_send()
-
-
-@functools.cache
-def order_of():
-    keys = [("p", "p", k) for k in range(2 * STEPS + 1)]
-    keys += [("p", "r", k) for k in range(2 * STEPS)]
-    keys += [("r", "r", k) for k in range(2 * STEPS - 1)]
-    return {key: index for index, key in enumerate(keys)}
-
-
-def hand_over(height, residual, out_height, out_residual):
-    out_height[...] = height[...]
-    out_residual[...] = residual[...]
+            results[which, at : at + 8, :] = total
+        if (at + 8) % SLAB == 0 or at + 8 == rows:
+            low = at // SLAB * SLAB
+            span = slice(low, at + 8)
+            for which, out in enumerate(outs):
+                pltpu.make_async_copy(
+                    results.at[which, span], out.at[span], out_sem.at[which]
+                ).start()
+    for which, out in enumerate(outs):
+        pltpu.make_async_copy(results.at[which], out, out_sem.at[which]).wait()
 
 
 def per_device(n_lat, n_lon, forcing, search_direction, ocean_depth, land_mask, fold_map):
@@ -928,17 +958,18 @@
     block = pl.BlockSpec(memory_space=pltpu.VMEM)
     outs = pl.pallas_call(
         functools.partial(kernel, n_lat, n_lon),
-        out_shape=[pltpu.VMEM((rows, width), f32)] * 2,
+        out_shape=[
+            tile(rows)[-1], tile(seam_rows)[-1], pltpu.VMEM((8, width), f32)
+        ],
         in_specs=[pl.BlockSpec(memory_space=pl.ANY)] * 5,
-        out_specs=[block] * 2,
+        out_specs=[block] * 3,
         scratch_shapes=[
             pltpu.VMEM((3, rows, width), f32), pltpu.VMEM((rows, width), jnp.int32),
             pltpu.SMEM(fold_map.shape, jnp.int32),
             pltpu.VMEM((3, tall, width), f32), pltpu.VMEM((3, tall, width), f32),
-            *tile(rows),
-            *tile(seam_rows),
+            *tile(rows)[:-1],
+            *tile(seam_rows)[:-1],
             *tile(max(group_rows + 2 * MARGIN, 2 * BAND)),
-            pltpu.VMEM((2, seam_rows, width), f32),
             edge, edge, edge,
             pltpu.VMEM((2, group_rows, width), f32),
             pltpu.VMEM((2, 3 * LIP + 2 * STEPS, width), f32),
@@ -950,20 +981,28 @@
             pltpu.VMEM((7 * LIP, width), f32),
             pltpu.VMEM((3, BAND, width), f32), pltpu.VMEM((3, BAND, width), f32),
             pltpu.VMEM((6 * STEPS, 8, width), f32),
-            pltpu.VMEM((6 * STEPS, width), f32),
             dma((3,)), dma((10,)), dma((11,)),
             *moment_refs,
         ],
         compiler_params=pltpu.CompilerParams(collective_id=0, has_side_effects=True),
         name="tripole_cg",
     )(forcing, search_direction, ocean_depth, land_mask, fold_map)
+    wide_basis, seam_basis, sums = (
+        pltpu.with_memory_space_constraint(out, pltpu.VMEM) for out in outs
+    )
     return pl.pallas_call(
-        hand_over,
+        finish,
         out_shape=[jax.ShapeDtypeStruct((rows, width), f32)] * 2,
-        in_specs=[block] * 2,
-        out_specs=[block] * 2,
-        name="hand_over",
-    )(*(pltpu.with_memory_space_constraint(out, pltpu.VMEM) for out in outs))
+        in_specs=[block] * 3,
+        out_specs=[pl.BlockSpec(memory_space=pl.ANY)] * 2,
+        scratch_shapes=[
+            pltpu.VMEM((6 * STEPS, width), f32),
+            pltpu.VMEM((2, seam_rows, width), f32),
+            pltpu.VMEM((2, rows, width), f32),
+            dma((2,)),
+        ],
+        name="finish",
+    )(sums, wide_basis, seam_basis)
 
 
 def solution(mesh):

time: 18.8 us -> 18.6 us (0.989)
  Pallas kernels: 18 us -> 17.8 us
    pallas_call x2, Pallas kernels: 18 us -> 17.8 us  [the longest x1 16.3 us: per_device(): pl.pallas_call(functools.partial(kernel, n_lat, n_lon), out_shape=[tile(r...]
where the time goes in v5:
time: 18.6 us; the launch traced here: 18.4 us
  Pallas kernels  17.8 us (96%)
  between operations  0.64 us (3%)
    pallas_call x1, Pallas kernels, per_device(): pl.pallas_call(functools.partial(kernel, n_lat, n_lon), out_shape=[tile(r...  16.3 us
    pallas_call x1, Pallas kernels, per_device(): pl.pallas_call(finish, out_shape=[jax.ShapeDtypeStruct((rows, width), f32...  1.46 us

profile of v5, /device:TPU:0, one launch (start us, length us, event | category | flops | bytes accessed | tf_op | source)
XLA Modules:
  0.0 18.4 jit_solution(3809326899322734215)
XLA Ops:
  0.6 16.3 %tripole_cg.1 = (f32[17,176,128]{2,1,0:T(8,128)S(1)}, f32[17,184,128]{2,1,0:T(8,128)S(1)}, f32[8,128]{1,0:T(8,128)S(1)}) custom-call(f32[160,128]{1,0:T(8,128)} %forcing_hbm.1, f32[160,128]{1,0:T(8,128)} %search_hbm.1, f32[160,128]{1,0:T(8,128)} %depth_hbm.1, s32[160,128]{1,0:T(8,128)} %mask_hbm.1, s32[1024]{0:T(1024)} %fold_hbm.1), custom_call_target="tpu_custom_call" | custom-call | tf_op jit(solution)/shard_map/tripole_cg/pallas_call | solution.py:959
  16.9 1.5 %finish.1 = (f32[160,128]{1,0:T(8,128)}, f32[160,128]{1,0:T(8,128)}) custom-call(f32[8,128]{1,0:T(8,128)S(1)} %get-tuple-element.5.sums, f32[17,176,128]{2,1,0:T(8,128)S(1)} %get-tuple-element.6.wide_basis, f32[17,184,128]{2,1,0:T(8,128)S(1)} %get-tuple-element.7.seam_basis), custom_call_target="tpu_custom_call" | custom-call | tf_op jit(solution)/shard_map/finish/pallas_call | solution.py:993

commit v6 on v5

--- a/solution.py
+++ b/solution.py
@@ -148,53 +148,52 @@
     return masks
 
 
-def prepare(rows, depth_root, shifted, weights, basis):
-    width = depth_root.shape[2]
+def gathered(around):
+    beside = around[-1] + around[1]
+    edge = around[0] + 0.5 * beside
+    return beside + (turned(edge, -1) + turned(edge, 1))
+
+
+def rows_near(ref, at, count):
+    return {a: ref[at + a : at + a + count, :] for a in (-1, 0, 1)}
+
+
+def clear(rows, planes, deep, basis):
+    width = planes.shape[2]
     zero = jnp.zeros((8, width), jnp.float32)
     for at in (0, 8 + rows):
-        span = pl.ds(at, 8)
-        depth_root[0, span, :] = zero
-        depth_root[1, span, :] = zero
+        planes[0, at : at + 8, :] = zero
+    for at in range(0, rows + 16, 8):
+        for slot in range(4):
+            deep[slot, at : at + 8, :] = zero
         for slot in range(2 * STEPS + 1):
-            if slot not in (STEPS, 2 * STEPS):
-                basis[slot, span, :] = zero
-
-    depth, root = depth_root.at[0], depth_root.at[1]
-    for at, count in chunks_of(0, rows + 16, CHUNK):
+            basis[slot, at : at + 8, :] = zero
+
+
+def prepare(rows, planes, deep, basis, regions):
+    depth = planes.at[0]
+    for at, count in chunks_of(8, 8 + rows, CHUNK):
         span = pl.ds(at, count)
-        shifted[0, span, :] = turned(depth[span, :], -1)
-        shifted[1, span, :] = turned(depth[span, :], 1)
-    shifted_depth = {0: depth, 1: shifted.at[0], -1: shifted.at[1]}
-    for at, count in chunks_of(8, 8 + rows, CHUNK):
-        here = depth[at : at + count, :]
-        sums = {0.5: None, 0.25: None}
-        for a, b in DIRECTIONS:
-            beside = shifted_depth[b][at + a : at + a + count, :]
-            link = jnp.where(beside > 0.0, here + beside, 0.0)
-            factor = halves((a, b))
-            sums[factor] = link if sums[factor] is None else sums[factor] + link
-        diagonal = here * (1.0 / (REACH * REACH)) + (0.5 * sums[0.5] + 0.25 * sums[0.25])
-        value = lax.rsqrt(jnp.where(here > 0.0, diagonal, 1.0))
-        span = pl.ds(at, count)
-        root[span, :] = value
-        shifted[2, span, :] = turned(value, -1)
-        shifted[3, span, :] = turned(value, 1)
-    shifted_root = {0: root, 1: shifted.at[2], -1: shifted.at[3]}
-    for at, count in chunks_of(8, 8 + rows, CHUNK):
-        for b in (-1, 0, 1):
-            goal_depth = shifted_depth[-b][at : at + count, :]
-            goal_root = shifted_root[-b][at : at + count, :]
-            for a in (-1, 0, 1):
-                if (a, b) == (0, 0):
-                    continue
-                from_depth = depth[at + a : at + a + count, :]
-                from_root = root[at + a : at + a + count, :]
-                link = jnp.where(
-                    jnp.minimum(goal_depth, from_depth) > 0.0, goal_depth + from_depth, 0.0
+        around = rows_near(depth, at, count)
+        here = around[0]
+        is_wet = here > 0.0
+        wet = {a: jnp.where(value > 0.0, 1.0, 0.0) for a, value in around.items()}
+        links = 0.5 * (here * gathered(wet) + gathered(around))
+        diagonal = jnp.where(is_wet, here * (1.0 / (REACH * REACH)) + links, 1.0)
+        root = lax.rsqrt(diagonal)
+        planes[3, span, :] = turned(here, 1)
+        planes[4, span, :] = turned(here, -1)
+        planes[1, span, :] = jnp.where(is_wet, -(root * root), 0.0)
+        basis[2 * STEPS + 1, span, :] = diagonal * root
+        for i, mask in enumerate(kept(at - 8, count, regions)):
+            if mask is not None:
+                planes[2, at + 8 * i : at + 8 * i + 8, :] = jnp.where(
+                    mask, diagonal[8 * i : 8 * i + 8, :], 0.0
                 )
-                weights[SLOT[(a, b)], at : at + count, :] = (
-                    goal_root * (-2.0 * halves((a, b)))
-                ) * (link * from_root)
+        for chain, slot in enumerate((0, STEPS + 1)):
+            value = root * basis[slot, span, :]
+            basis[slot, span, :] = value
+            deep[chain, span, :] = here * value
 
 
 def needed(rows, regions, reach):
@@ -212,13 +211,12 @@
     return [(8 + at, count) for at, count in runs]
 
 
-def march(rows, weights, basis, regions, add_dot, flush, new):
-    def keep(at, count):
-        return kept(at, count, regions)
-
-    def masked(masks, value):
+def march(rows, planes, deep, basis, regions, add_dot, flush, new):
+    def weighted(at, masks, value):
         return [
-            None if mask is None else jnp.where(mask, value[8 * i : 8 * i + 8, :], 0.0)
+            None
+            if mask is None
+            else planes[2, at + 8 * i : at + 8 * i + 8, :] * value[8 * i : 8 * i + 8, :]
             for i, mask in enumerate(masks)
         ]
 
@@ -230,8 +228,8 @@
     for at, count in needed(rows, regions, 0) if add_dot else []:
         p0 = basis[0, at : at + count, :]
         r0 = basis[STEPS + 1, at : at + count, :]
-        masks = keep(at - 8, count)
-        p0_kept, r0_kept = masked(masks, p0), masked(masks, r0)
+        masks = kept(at - 8, count, regions)
+        p0_kept, r0_kept = weighted(at, masks, p0), weighted(at, masks, r0)
         dot(("p", "p", 0), p0_kept, p0)
         dot(("r", "r", 0), r0_kept, r0)
         dot(("p", "r", 0), p0_kept, r0)
@@ -241,31 +239,34 @@
         for at, count in needed(rows, regions, STEPS - power):
             fresh = {}
             held = {}
-            factors = {ab: weights[SLOT[ab], at : at + count, :] for ab in DIRECTIONS}
-            for name, origin in chains:
+            depth, factor, west_depth, east_depth = (
+                planes[plane, at : at + count, :] for plane in (0, 1, 3, 4)
+            )
+            for chain, (name, origin) in enumerate(chains):
                 slot = origin + power
-                taken = {a: basis[slot - 1, at + a : at + a + count, :] for a in (-1, 0, 1)}
+                before, after = (power + 1) % 2 * 2 + chain, power % 2 * 2 + chain
+                taken = rows_near(basis.at[slot - 1], at, count)
                 held[name] = taken[0]
-                columns = {}
-                for b in (-1, 0, 1):
-                    total = None
-                    for a in (-1, 0, 1):
-                        if (a, b) == (0, 0):
-                            continue
-                        term = factors[(a, b)] * taken[a]
-                        total = term if total is None else total + term
-                    columns[b] = total
-                value = columns[0] + turned(columns[1], -1) + turned(columns[-1], 1)
+                heavy = rows_near(deep.at[before], at, count)
+                beside, beside_heavy = taken[-1] + taken[1], heavy[-1] + heavy[1]
+                edge = taken[0] + 0.5 * beside
+                edge_heavy = heavy[0] + 0.5 * beside_heavy
+                sums = (depth * beside + beside_heavy) + (
+                    turned(west_depth * edge + edge_heavy, -1)
+                    + turned(east_depth * edge + edge_heavy, 1)
+                )
                 if power == 1:
-                    value = 0.5 * value
+                    value = (0.5 * factor) * sums
                 else:
-                    value = value - basis[slot - 2, at : at + count, :]
+                    value = factor * sums - basis[slot - 2, at : at + count, :]
                 basis[slot, at : at + count, :] = value
+                if power < STEPS:
+                    deep[after, at : at + count, :] = depth * value
                 fresh[name] = value
             if not add_dot:
                 continue
-            masks = keep(at - 8, count)
-            fresh_kept = {name: masked(masks, fresh[name]) for name, _ in chains}
+            masks = kept(at - 8, count, regions)
+            fresh_kept = {name: weighted(at, masks, fresh[name]) for name, _ in chains}
             for name, _ in chains:
                 dot((name, name, 2 * power), fresh_kept[name], fresh[name])
                 dot((name, name, 2 * power - 1), fresh_kept[name], held[name])
@@ -285,8 +286,7 @@
 def kernel(
     n_lat, n_lon, forcing_hbm, search_hbm, depth_hbm, mask_hbm, fold_hbm,
     wide_basis, seam_basis, sums_out, loaded, mask_in, fold_map,
-    centre, side, wide, wide_shifted, wide_weights, seam, seam_shifted,
-    seam_weights, far, far_shifted, far_weights, far_basis, row_north, row_south,
+    centre, side, wide, wide_deep, seam, seam_deep, far, far_deep, far_basis, row_north, row_south,
     fold_rows, packed, got_rows, got_sides, fold_all, deep_packed, got_deep, deep_rows, got_far,
     far_centre, far_side, dots, load_sem, near_send, near_recv, *moment_refs,
 ):
@@ -326,6 +326,15 @@
             greet(place)
         greeted = n_lat - 1 + n_lon - 1 + 4
 
+    n_parts = width // GROUP // 2
+    part_rows = rows // n_parts
+    strip_rows = part_rows + 2 * MARGIN
+    seam_rows = strip_rows + 2 * BAND
+    patch_rows = group_rows + 2 * MARGIN
+    far_tile_rows = max(patch_rows, 2 * BAND)
+    clear(rows, wide, wide_deep, wide_basis)
+    clear(seam_rows, seam, seam_deep, seam_basis)
+    clear(far_tile_rows, far, far_deep, far_basis)
     pltpu.make_async_copy(mask_hbm, mask_in, load_sem.at[0]).wait()
     pltpu.make_async_copy(loaded, loaded, load_sem.at[1]).wait()
     pltpu.make_async_copy(fold_hbm, fold_map, load_sem.at[2]).wait()
@@ -523,12 +532,11 @@
     lane8 = lax.broadcasted_iota(jnp.int32, (8, width), 1)
     nothing = jnp.zeros((8, width), jnp.float32)
 
-    prepare(rows, wide, wide_shifted, wide_weights, wide_basis)
     middle = (lane8 >= LIP) & (lane8 < width - LIP)
 
-    march(
-        rows, wide_weights, wide_basis, [(LIP, rows - LIP, middle)], add_dot, flush, True
-    )
+    wide_regions = [(LIP, rows - LIP, middle)]
+    prepare(rows, wide, wide_deep, wide_basis, wide_regions)
+    march(rows, wide, wide_deep, wide_basis, wide_regions, add_dot, flush, True)
 
     part_spans = ((0, 0, LIP), (1, LIP, STEPS), (2, LIP + STEPS, STEPS))
 
@@ -600,15 +608,27 @@
             for index, at, count in spans:
                 target[index, last : last + count, :] = source[at : at + count, :]
 
-    n_parts = width // GROUP // 2
-    part_rows = rows // n_parts
-    strip_rows = part_rows + 2 * MARGIN
-    seam_rows = strip_rows + 2 * BAND
     north_at, south_at = strip_rows, strip_rows + BAND
     own = GROUP - LIP
     slot_of = lane8 // GROUP
     slot_lane = lane8 - slot_of * GROUP
 
+    east_half = lane8 < n_parts * GROUP
+    strip_at = jnp.where(east_half, slot_lane - (own - LIP), slot_lane - LIP)
+    closed = jnp.where(fold_late, 1, 0)
+    strip_lanes = (strip_at >= 0) & (strip_at < LIP) & (
+        jnp.where(east_half, lon, -1) < n_lon - 1
+    )
+    last_part = lax.rem(slot_of, n_parts) == n_parts - 1
+    north_lanes = strip_lanes & (jnp.where(last_part, closed, 0) == 0)
+    band_lanes = jnp.where(middle, closed, 1) == 0
+
+    seam_regions = [
+        (MARGIN, MARGIN + part_rows - LIP, strip_lanes),
+        (MARGIN + part_rows - LIP, MARGIN + part_rows, north_lanes),
+        (north_at + BAND - 2 * LIP, north_at + BAND - LIP, band_lanes),
+        (south_at + LIP, south_at + 2 * LIP, middle),
+    ]
     def assemble():
         targets = (seam.at[0], seam_basis.at[0], seam_basis.at[STEPS + 1])
         for index, target in enumerate(targets):
@@ -634,7 +654,7 @@
                 target[8 + north_at + at : 16 + north_at + at, :] = centre[index, low : low + 8, :]
                 low = first - LIP + at
                 target[8 + south_at + at : 16 + south_at + at, :] = centre[index, low : low + 8, :]
-        prepare(seam_rows, seam, seam_shifted, seam_weights, seam_basis)
+        prepare(seam_rows, seam, seam_deep, seam_basis, seam_regions)
 
     arrival(2, got_west).wait_recv()
     for g in range(n_groups):
@@ -663,31 +683,13 @@
         take_fold()
 
     assemble()
-    east_half = lane8 < n_parts * GROUP
-    strip_at = jnp.where(east_half, slot_lane - (own - LIP), slot_lane - LIP)
-    closed = jnp.where(fold_late, 1, 0)
-    strip_lanes = (strip_at >= 0) & (strip_at < LIP) & (
-        jnp.where(east_half, lon, -1) < n_lon - 1
-    )
-    last_part = lax.rem(slot_of, n_parts) == n_parts - 1
-    north_lanes = strip_lanes & (jnp.where(last_part, closed, 0) == 0)
-    band_lanes = jnp.where(middle, closed, 1) == 0
-
-    seam_regions = [
-        (MARGIN, MARGIN + part_rows - LIP, strip_lanes),
-        (MARGIN + part_rows - LIP, MARGIN + part_rows, north_lanes),
-        (north_at + BAND - 2 * LIP, north_at + BAND - LIP, band_lanes),
-        (south_at + LIP, south_at + 2 * LIP, middle),
-    ]
-    march(seam_rows, seam_weights, seam_basis, seam_regions, add_dot, flush, False)
-
-    patch_rows = group_rows + 2 * MARGIN
-    far_tile_rows = max(patch_rows, 2 * BAND)
+    march(seam_rows, seam, seam_deep, seam_basis, seam_regions, add_dot, flush, False)
+
     far_targets = (far.at[0], far_basis.at[0], far_basis.at[STEPS + 1])
 
     def march_far(regions):
-        prepare(far_tile_rows, far, far_shifted, far_weights, far_basis)
-        march(far_tile_rows, far_weights, far_basis, regions, add_dot, flush, False)
+        prepare(far_tile_rows, far, far_deep, far_basis, regions)
+        march(far_tile_rows, far, far_deep, far_basis, regions, add_dot, flush, False)
 
     @pl.when(past_seam)
     def _():
@@ -780,7 +782,7 @@
                 take_fold()
 
             assemble()
-            march(seam_rows, seam_weights, seam_basis, seam_regions, None, None, False)
+            march(seam_rows, seam, seam_deep, seam_basis, seam_regions, None, None, False)
 
     number = len(order_of())
     pending = []
@@ -898,11 +900,14 @@
                 if (chain, power) in coords:
                     term = coords[(chain, power)] * field
                     totals[which] = term if totals[which] is None else totals[which] + term
-        return totals
-
-    for at in range(0, seam_rows, 8):
-        for which, total in enumerate(combined(seam_basis, at)):
-            patch[which, at : at + 8, :] = total
+        stretch = fields[2 * STEPS + 1, 8 + at : 16 + at, :]
+        return [stretch * total for total in totals]
+
+    kept_rows = ((MARGIN, part_rows), (north_at + BAND - 2 * LIP, LIP), (south_at + LIP, LIP))
+    for start, count in needed(seam_rows, [(low, low + size, None) for low, size in kept_rows], 0):
+        for at in range(start - 8, start - 8 + count, 8):
+            for which, total in enumerate(combined(seam_basis, at)):
+                patch[which, at : at + 8, :] = total
     row8 = lax.broadcasted_iota(jnp.int32, (8, width), 0)
     for at in range(0, rows, 8):
         q = at // part_rows
@@ -945,7 +950,7 @@
     def tile(count):
         return [
             pltpu.VMEM((planes, count + 16, width), f32)
-            for planes in (2, 4, 8, 2 * STEPS + 1)
+            for planes in (5, 4, 2 * STEPS + 2)
         ]
 
     edge = pltpu.VMEM((32, width), f32)

time: 18.6 us -> 18.2 us (0.978)
  Pallas kernels: 17.8 us -> 17.4 us
    pallas_call x1, Pallas kernels: 16.3 us -> 16 us  [per_device(): pl.pallas_call(functools.partial(kernel, n_lat, n_lon), out_shape=[tile(r...]
where the time goes in v6:
time: 18.2 us; the launch traced here: 18 us
  Pallas kernels  17.4 us (96%)
  between operations  0.64 us (4%)
    pallas_call x1, Pallas kernels, per_device(): pl.pallas_call(functools.partial(kernel, n_lat, n_lon), out_shape=[tile(r...  16 us
    pallas_call x1, Pallas kernels, per_device(): pl.pallas_call(finish, out_shape=[jax.ShapeDtypeStruct((rows, width), f32...  1.4 us

profile of v6, /device:TPU:0, one launch (start us, length us, event | category | flops | bytes accessed | tf_op | source)
XLA Modules:
  0.0 18.0 jit_solution(4410328534413137417)
XLA Ops:
  0.6 16.0 %tripole_cg.1 = (f32[18,176,128]{2,1,0:T(8,128)S(1)}, f32[18,184,128]{2,1,0:T(8,128)S(1)}, f32[8,128]{1,0:T(8,128)S(1)}) custom-call(f32[160,128]{1,0:T(8,128)} %forcing_hbm.1, f32[160,128]{1,0:T(8,128)} %search_hbm.1, f32[160,128]{1,0:T(8,128)} %depth_hbm.1, s32[160,128]{1,0:T(8,128)} %mask_hbm.1, s32[1024]{0:T(1024)} %fold_hbm.1), custom_call_target="tpu_custom_call" | custom-call | tf_op jit(solution)/shard_map/tripole_cg/pallas_call | solution.py:964
  16.6 1.4 %finish.1 = (f32[160,128]{1,0:T(8,128)}, f32[160,128]{1,0:T(8,128)}) custom-call(f32[8,128]{1,0:T(8,128)S(1)} %get-tuple-element.5.sums, f32[18,176,128]{2,1,0:T(8,128)S(1)} %get-tuple-element.6.wide_basis, f32[18,184,128]{2,1,0:T(8,128)S(1)} %get-tuple-element.7.seam_basis), custom_call_target="tpu_custom_call" | custom-call | tf_op jit(solution)/shard_map/finish/pallas_call | solution.py:998

commit v7 on v6

--- a/solution.py
+++ b/solution.py
@@ -384,10 +384,10 @@
 
     pl.semaphore_wait(barrier, greeted)
 
-    half = n_lon // 2
+    reach = n_lon // 2 + 1
     at_seam, past_seam = lon == n_lon - 1, lon == 0
     on_top = lat == top
-    fold_late, fold_early = on_top & (lon > half), on_top & (lon >= 1) & (lon < half)
+    fold_late, fold_early = on_top & (lon > reach), on_top & (lon >= 1) & (lon < n_lon - reach)
 
     def near(gone, arrived, source, target, place):
         return pltpu.make_async_remote_copy(
@@ -429,14 +429,14 @@
     deep_up = near(5, 8, deep_packed.at[tail], deep_south, (north, east))
     deep_down = near(6, 9, deep_packed.at[head], deep_north, (south, east))
 
-    def across_half(step):
+    def at_reach(step):
         return (lat, lax.rem(lon + step + n_lon, n_lon))
 
-    far_away = near(7, 10, deep_rows, far_rows, across_half(-half))
-    far_west_edge = near(8, 10, packed.at[1, tall_tail], far_edges[0], across_half(1 - half))
-    far_east_edge = near(9, 10, packed.at[0, tall_tail], far_edges[1], across_half(-1 - half))
-    gives_west_edge = on_top & (lon >= half) & (lon < n_lon - 1)
-    gives_east_edge = on_top & ((lon > half + 1) | (lon == 0))
+    far_away = near(7, 10, deep_rows, far_rows, at_reach(-reach))
+    far_west_edge = near(8, 10, packed.at[1, tall_tail], far_edges[0], at_reach(1 - reach))
+    far_east_edge = near(9, 10, packed.at[0, tall_tail], far_edges[1], at_reach(-1 - reach))
+    gives_west_edge = on_top & (lon >= reach) & (lon < n_lon - 1)
+    gives_east_edge = on_top & ((lon > reach + 1) | (lon == 0))
 
     def spread(source, slot, send_sem, recv_sem, along_lat):
         size = n_lat if along_lat else n_lon
@@ -678,7 +678,7 @@
     def _():
         take_east()
 
-    @pl.when(on_top & (lon <= half))
+    @pl.when(on_top & (lon <= reach))
     def _():
         take_fold()
 
@@ -738,7 +738,7 @@
                 for at in range(0, BAND, 8):
                     target[index, at : at + 8, :] = nothing
         arrival(10, got_far).wait_recv()
-        home = lon + half
+        home = lon + reach
         low = edge_row - 2 * LIP
         unpack_west(far_edges[0][...], far_side, low, n_groups - 1, 2 * LIP)
         unpack_east(far_edges[1][...], far_side, low, n_groups - 1, 2 * LIP)

time: 18.2 us -> 18.2 us (level)
  no operation moved by 1% of the time
where the time goes in v7:
time: 18.2 us; the launch traced here: 18 us
  Pallas kernels  17.4 us (96%)
  between operations  0.64 us (4%)
    pallas_call x1, Pallas kernels, per_device(): pl.pallas_call(functools.partial(kernel, n_lat, n_lon), out_shape=[tile(r...  16 us
    pallas_call x1, Pallas kernels, per_device(): pl.pallas_call(finish, out_shape=[jax.ShapeDtypeStruct((rows, width), f32...  1.4 us

profile of v7, /device:TPU:0, one launch (start us, length us, event | category | flops | bytes accessed | tf_op | source)
XLA Modules:
  0.0 18.0 jit_solution(9680961072684042040)
XLA Ops:
  0.6 16.0 %tripole_cg.1 = (f32[18,176,128]{2,1,0:T(8,128)S(1)}, f32[18,184,128]{2,1,0:T(8,128)S(1)}, f32[8,128]{1,0:T(8,128)S(1)}) custom-call(f32[160,128]{1,0:T(8,128)} %forcing_hbm.1, f32[160,128]{1,0:T(8,128)} %search_hbm.1, f32[160,128]{1,0:T(8,128)} %depth_hbm.1, s32[160,128]{1,0:T(8,128)} %mask_hbm.1, s32[1024]{0:T(1024)} %fold_hbm.1), custom_call_target="tpu_custom_call" | custom-call | tf_op jit(solution)/shard_map/tripole_cg/pallas_call | solution.py:964
  16.6 1.4 %finish.1 = (f32[160,128]{1,0:T(8,128)}, f32[160,128]{1,0:T(8,128)}) custom-call(f32[8,128]{1,0:T(8,128)S(1)} %get-tuple-element.5.sums, f32[18,176,128]{2,1,0:T(8,128)S(1)} %get-tuple-element.6.wide_basis, f32[18,184,128]{2,1,0:T(8,128)S(1)} %get-tuple-element.7.seam_basis), custom_call_target="tpu_custom_call" | custom-call | tf_op jit(solution)/shard_map/finish/pallas_call | solution.py:998
